TPU v7x, 32 devices: a whole 2x2x4 slice. The times are simulated.
32 devices in a mesh: dp: 8 (over y, x, core), seq: 4 (over z).
Axes of the slice: x: 2, y: 2, z: 4, core: 2. Of those that a mesh axis runs over, the one named last changes fastest.
Arguments:
- tokens: bfloat16 [16, 1024, 1024], P('dp', 'seq'), may hold values from -16 to 16
- condition: bfloat16 [16, 1024], P('dp'), may hold values from -6 to 6
- ada_weight: bfloat16 [1024, 6144], P('dp'), may hold values from -0.1875 to 0.1875
- ada_bias: bfloat16 [6144], P('dp'), may hold values from -3 to 3
- qkv_weight: bfloat16 [1024, 3072], P('dp'), may hold values from -4 to 4
- qv_bias: bfloat16 [2048], P('dp'), may hold values from -3 to 3
- out_weight: bfloat16 [1024, 1024], P('dp'), may hold values from -0.75 to 0.75
- out_bias: bfloat16 [1024], P('dp'), may hold values from -3 to 3
- up_weight: bfloat16 [1024, 4096], P('dp'), may hold values from -0.1875 to 0.1875
- up_bias: bfloat16 [4096], P('dp'), may hold values from -3 to 3
- down_weight: bfloat16 [4096, 1024], P('dp'), may hold values from -0.09375 to 0.09375
- down_bias: bfloat16 [1024], P('dp'), may hold values from -3 to 3
- cotangent: bfloat16 [16, 1024, 1024], P('dp', 'seq'), may hold values from -6 to 6
Outputs:
- output: bfloat16 [16, 1024, 1024], P('dp', 'seq')
- tokens_grad: float32 [16, 1024, 1024], P('dp', 'seq')
- condition_grad: float32 [16, 1024], P('dp')
- ada_weight_grad: float32 [1024, 6144], P('dp')
- ada_bias_grad: float32 [6144], P('dp')
- qkv_weight_grad: float32 [1024, 3072], P('dp')
- qv_bias_grad: float32 [2048], P('dp')
- out_weight_grad: float32 [1024, 1024], P('dp')
- out_bias_grad: float32 [1024], P('dp')
- up_weight_grad: float32 [1024, 4096], P('dp')
- up_bias_grad: float32 [4096], P('dp')
- down_weight_grad: float32 [4096, 1024], P('dp')
- down_bias_grad: float32 [1024], P('dp')
All inputs are finite; a program needn't handle non-finite values.
Results may differ from a plain program's by a relative error of at most 0.012.
The roundings to bfloat16 on the way count: a program that leaves them out, or rounds other values in their place, can miss the bound.
Values may be sent and summed in bfloat16 or wider, within the bound.
A program may use at most 256 MiB of HBM per device.

v0:
```python
import jax
import jax.numpy as jnp
from jax import lax
from jax.sharding import PartitionSpec as P

HD = 64


EPSILON = 1e-06


def norm_shift(inputs, shift_row, scale_row):
    centred = inputs - jnp.mean(inputs, axis=-1, keepdims=True)
    variance = jnp.mean(centred * centred, axis=-1, keepdims=True)
    return centred * lax.rsqrt(variance + EPSILON) * (1.0 + scale_row) + shift_row


def gelu_tanh(inputs):
    return jax.nn.gelu(inputs, approximate=True)


def head_parts(head_block):
    length = head_block.shape[0]
    part_width = head_block.shape[-1]
    head_count = part_width // HD
    query_part = head_block[:, 0].reshape(length, head_count, HD)
    key_part = head_block[:, 1].reshape(length, head_count, HD)
    value_part = head_block[:, 2].reshape(length, head_count, HD)
    return (query_part, key_part, value_part)


def attend_block(head_block):
    length = head_block.shape[0]
    part_width = head_block.shape[-1]
    query_part, key_part, value_part = head_parts(head_block)
    scores = jnp.einsum(
        "qhd,khd->hqk", query_part, key_part, preferred_element_type=jnp.float32
    ) * HD ** (-0.5)
    row_peak = jnp.max(scores, axis=-1, keepdims=True)
    logsum = row_peak[..., 0] + jnp.log(jnp.sum(jnp.exp(scores - row_peak), axis=-1))
    attn_probs = jnp.exp(scores - logsum[..., None]).astype(jnp.bfloat16)
    mixed_rows = jnp.einsum(
        "hqk,khd->qhd", attn_probs, value_part, preferred_element_type=jnp.float32
    )
    return (mixed_rows.reshape(length, part_width).astype(jnp.bfloat16), logsum)


def attend_items(head_blocks):
    mixed_rows, logsum = lax.map(attend_block, head_blocks)
    return (mixed_rows, logsum, head_blocks)


def attend_grad(inputs):
    head_block, logsum, grad_rows = inputs
    length = head_block.shape[0]
    part_width = head_block.shape[-1]
    query_part, key_part, value_part = head_parts(head_block)
    grad_part = grad_rows.reshape(length, part_width // HD, HD)
    scale_value = HD ** (-0.5)
    scores = (
        jnp.einsum("qhd,khd->hqk", query_part, key_part, preferred_element_type=jnp.float32)
        * scale_value
    )
    attn_probs = jnp.exp(scores - logsum[..., None])
    probs_half = attn_probs.astype(jnp.bfloat16)
    grad_value = jnp.einsum(
        "hqk,qhd->khd", probs_half, grad_part, preferred_element_type=jnp.float32
    )
    grad_probs = jnp.einsum(
        "qhd,khd->hqk", grad_part, value_part, preferred_element_type=jnp.float32
    )
    inner_sum = jnp.sum(attn_probs * grad_probs, axis=-1, keepdims=True)
    grad_scores = (attn_probs * (grad_probs - inner_sum) * scale_value).astype(jnp.bfloat16)
    grad_query = jnp.einsum(
        "hqk,khd->qhd", grad_scores, key_part, preferred_element_type=jnp.float32
    )
    grad_key = jnp.einsum(
        "hqk,qhd->khd", grad_scores, query_part, preferred_element_type=jnp.float32
    )
    stacked = jnp.stack(
        [
            grad_query.reshape(length, part_width),
            grad_key.reshape(length, part_width),
            grad_value.reshape(length, part_width),
        ],
        axis=1,
    )
    return stacked.astype(jnp.bfloat16)


def body(
    tokens,
    condition,
    ada_weight,
    ada_bias,
    qkv_weight,
    qv_bias,
    out_weight,
    out_bias,
    up_weight,
    up_bias,
    down_weight,
    down_bias,
    cotangent,
):
    lat_count, seq_part, model_width = tokens.shape
    cond_float = condition.astype(jnp.float32)
    silu_cond = jax.nn.silu(cond_float).astype(jnp.bfloat16)
    (
        ada_full,
        ada_bias_full,
        qkv_full,
        qv_full,
        out_full,
        out_bias_full,
        up_full,
        up_bias_full,
        down_full,
        down_bias_full,
    ) = (
        lax.all_gather(ada_weight, "dp", axis=0, tiled=True),
        lax.all_gather(ada_bias, "dp", axis=0, tiled=True),
        lax.all_gather(qkv_weight, "dp", axis=0, tiled=True),
        lax.all_gather(qv_bias, "dp", axis=0, tiled=True),
        lax.all_gather(out_weight, "dp", axis=0, tiled=True),
        lax.all_gather(out_bias, "dp", axis=0, tiled=True),
        lax.all_gather(up_weight, "dp", axis=0, tiled=True),
        lax.all_gather(up_bias, "dp", axis=0, tiled=True),
        lax.all_gather(down_weight, "dp", axis=0, tiled=True),
        lax.all_gather(down_bias, "dp", axis=0, tiled=True),
    )
    modulation = jnp.dot(
        silu_cond, ada_full, preferred_element_type=jnp.float32
    ) + ada_bias_full.astype(jnp.float32)
    mod_pieces = modulation.reshape(lat_count, 6, 1, model_width)
    shift_a, scale_a, gate_a = (mod_pieces[:, 0], mod_pieces[:, 1], mod_pieces[:, 2])
    shift_b, scale_b, gate_b = (mod_pieces[:, 3], mod_pieces[:, 4], mod_pieces[:, 5])
    tokens_float = tokens.astype(jnp.float32)
    normed_a = norm_shift(tokens_float, shift_a, scale_a).astype(jnp.bfloat16)
    flat_a = normed_a.reshape(-1, model_width)
    bias_all = jnp.concatenate(
        [qv_full[:model_width], jnp.zeros((model_width,), qv_full.dtype), qv_full[model_width:]]
    ).astype(jnp.float32)
    projected = (jnp.dot(flat_a, qkv_full, preferred_element_type=jnp.float32) + bias_all).astype(
        jnp.bfloat16
    )
    projected = projected.reshape(lat_count, seq_part, 3, model_width)
    mixed_heads, logsum, kept_heads = attend_items(
        lax.all_to_all(projected, "seq", split_axis=3, concat_axis=1, tiled=True)
    )
    attended = lax.all_to_all(mixed_heads, "seq", split_axis=1, concat_axis=2, tiled=True).reshape(
        -1, model_width
    )
    branch_a = (
        jnp.dot(attended, out_full, preferred_element_type=jnp.float32)
        + out_bias_full.astype(jnp.float32)
    ).reshape(lat_count, seq_part, model_width)
    middle = tokens_float + gate_a * branch_a
    normed_b = norm_shift(middle, shift_b, scale_b).astype(jnp.bfloat16)
    flat_b = normed_b.reshape(-1, model_width)
    hidden_pre = jnp.dot(flat_b, up_full, preferred_element_type=jnp.float32) + up_bias_full.astype(
        jnp.float32
    )
    hidden = gelu_tanh(hidden_pre).astype(jnp.bfloat16)
    branch_b = (
        jnp.dot(hidden, down_full, preferred_element_type=jnp.float32)
        + down_bias_full.astype(jnp.float32)
    ).reshape(lat_count, seq_part, model_width)
    output = (middle + gate_b * branch_b).astype(jnp.bfloat16)
    cot_float = cotangent.astype(jnp.float32)
    grad_gate_b = jnp.sum(cot_float * branch_b, axis=1, keepdims=True)
    grad_branch_b = (cot_float * gate_b).reshape(-1, model_width)
    down_bias_grad = jnp.sum(grad_branch_b, axis=0)
    grad_branch_half = grad_branch_b.astype(jnp.bfloat16)
    down_weight_grad = jnp.dot(hidden.T, grad_branch_half, preferred_element_type=jnp.float32)
    grad_hidden = jnp.dot(grad_branch_half, down_full.T, preferred_element_type=jnp.float32)
    _, gelu_back = jax.vjp(gelu_tanh, hidden_pre)
    grad_pre = gelu_back(grad_hidden)[0]
    up_bias_grad = jnp.sum(grad_pre, axis=0)
    grad_pre_half = grad_pre.astype(jnp.bfloat16)
    up_weight_grad = jnp.dot(flat_b.T, grad_pre_half, preferred_element_type=jnp.float32)
    grad_normed_b = jnp.dot(grad_pre_half, up_full.T, preferred_element_type=jnp.float32).reshape(
        lat_count, seq_part, model_width
    )
    _, norm_back_b = jax.vjp(norm_shift, middle, shift_b, scale_b)
    grad_mid_norm, grad_shift_b, grad_scale_b = norm_back_b(grad_normed_b)
    grad_middle = cot_float + grad_mid_norm
    grad_gate_a = jnp.sum(grad_middle * branch_a, axis=1, keepdims=True)
    grad_branch_a = (grad_middle * gate_a).reshape(-1, model_width)
    out_bias_grad = jnp.sum(grad_branch_a, axis=0)
    grad_branch_a_half = grad_branch_a.astype(jnp.bfloat16)
    out_weight_grad = jnp.dot(attended.T, grad_branch_a_half, preferred_element_type=jnp.float32)
    grad_attended = jnp.dot(
        grad_branch_a_half, out_full.T, preferred_element_type=jnp.float32
    ).astype(jnp.bfloat16)
    grad_attended = grad_attended.reshape(lat_count, seq_part, model_width)
    grad_head_rows = lax.all_to_all(grad_attended, "seq", split_axis=2, concat_axis=1, tiled=True)
    grad_blocks = lax.map(attend_grad, (kept_heads, logsum, grad_head_rows))
    grad_projected = lax.all_to_all(
        grad_blocks, "seq", split_axis=1, concat_axis=3, tiled=True
    ).reshape(-1, 3 * model_width)
    qkv_weight_grad = jnp.dot(flat_a.T, grad_projected, preferred_element_type=jnp.float32)
    grad_proj_float = grad_projected.astype(jnp.float32)
    qv_bias_grad = jnp.concatenate(
        [
            jnp.sum(grad_proj_float[:, :model_width], axis=0),
            jnp.sum(grad_proj_float[:, 2 * model_width :], axis=0),
        ]
    )
    grad_normed_a = jnp.dot(grad_projected, qkv_full.T, preferred_element_type=jnp.float32).reshape(
        lat_count, seq_part, model_width
    )
    _, norm_back_a = jax.vjp(norm_shift, tokens_float, shift_a, scale_a)
    grad_tok_norm, grad_shift_a, grad_scale_a = norm_back_a(grad_normed_a)
    tokens_grad = grad_middle + grad_tok_norm
    grad_mod_part = jnp.concatenate(
        [grad_shift_a, grad_scale_a, grad_gate_a, grad_shift_b, grad_scale_b, grad_gate_b], axis=-1
    ).reshape(lat_count, 6 * model_width)
    grad_modulation = lax.psum(grad_mod_part, "seq")
    grad_mod_half = grad_modulation.astype(jnp.bfloat16)
    sigmoid_cond = jax.nn.sigmoid(cond_float)
    silu_slope = sigmoid_cond * (1.0 + cond_float * (1.0 - sigmoid_cond))
    ada_weight_local = jnp.dot(silu_cond.T, grad_mod_half, preferred_element_type=jnp.float32)
    ada_bias_local = jnp.sum(grad_modulation, axis=0)
    condition_grad = silu_slope * jnp.dot(
        grad_mod_half, ada_full.T, preferred_element_type=jnp.float32
    )
    (
        ada_weight_grad,
        ada_bias_grad,
        share_qkv,
        share_qv,
        share_out,
        share_out_bias,
        share_up,
        share_up_bias,
        share_down,
        share_down_bias,
    ) = (
        lax.psum_scatter(ada_weight_local, "dp", scatter_dimension=0, tiled=True),
        lax.psum_scatter(ada_bias_local, "dp", scatter_dimension=0, tiled=True),
        lax.psum_scatter(qkv_weight_grad, "dp", scatter_dimension=0, tiled=True),
        lax.psum_scatter(qv_bias_grad, "dp", scatter_dimension=0, tiled=True),
        lax.psum_scatter(out_weight_grad, "dp", scatter_dimension=0, tiled=True),
        lax.psum_scatter(out_bias_grad, "dp", scatter_dimension=0, tiled=True),
        lax.psum_scatter(up_weight_grad, "dp", scatter_dimension=0, tiled=True),
        lax.psum_scatter(up_bias_grad, "dp", scatter_dimension=0, tiled=True),
        lax.psum_scatter(down_weight_grad, "dp", scatter_dimension=0, tiled=True),
        lax.psum_scatter(down_bias_grad, "dp", scatter_dimension=0, tiled=True),
    )
    reduced = lax.psum(
        (
            share_qkv,
            share_qv,
            share_out,
            share_out_bias,
            share_up,
            share_up_bias,
            share_down,
            share_down_bias,
        ),
        "seq",
    )
    return (
        output,
        tokens_grad,
        condition_grad,
        ada_weight_grad,
        ada_bias_grad,
        reduced[0],
        reduced[1],
        reduced[2],
        reduced[3],
        reduced[4],
        reduced[5],
        reduced[6],
        reduced[7],
    )


def solution(mesh):
    return jax.shard_map(
        body,
        mesh=mesh,
        in_specs=(
            P("dp", "seq", None),
            P("dp", None),
            P("dp", None),
            P("dp"),
            P("dp", None),
            P("dp"),
            P("dp", None),
            P("dp"),
            P("dp", None),
            P("dp"),
            P("dp", None),
            P("dp"),
            P("dp", "seq", None),
        ),
        out_specs=(
            P("dp", "seq", None),
            P("dp", "seq", None),
            P("dp", None),
            P("dp", None),
            P("dp"),
            P("dp", None),
            P("dp"),
            P("dp", None),
            P("dp"),
            P("dp", None),
            P("dp"),
            P("dp", None),
            P("dp"),
        ),
        check_vma=False,
    )
```

profile of v0, /device:TPU:0, one launch (start us, length us, event | category | flops | bytes accessed | tf_op | source)
XLA Modules:
  0.0 1312.1 jit_solution(9314472414217798720)
XLA Ops:
  10.7 10.6 all-gather
  21.9 9.2 all-gather.1
  31.9 52.8 %all-gather.11.cloned.1.call-done = bf16[1024,6144]{1,0:T(8,128)(2,1)} async-done(((bf16[128,6144]{1,0:T(8,128)(2,1)}), bf16[1024,6144]{1,0:T(8,128)(2,1)}) %all-gather.11.cloned.1.call-update) | async-done | bytes 12582928 | tf_op jit(solution)/shard_map/all_gather | solution.py:121
  91.6 40.3 %all-gather.13.cloned.1.call-done = bf16[1024,3072]{1,0:T(8,128)(2,1)} async-done(((bf16[128,3072]{1,0:T(8,128)(2,1)}), bf16[1024,3072]{1,0:T(8,128)(2,1)}) %all-gather.13.cloned.1.call-update) | async-done | bytes 6291472 | tf_op jit(solution)/shard_map/all_gather | solution.py:123
  139.5 10.1 reshape.299
  149.6 11.6 copy.91
  166.5 70.8 %all-to-all-done = bf16[2,256,3,1024]{1,0,2,3:T(2,128)(2,1)} async-done(((bf16[2,256,3,1024]{1,0,2,3:T(2,128)(2,1)}), bf16[2,256,3,1024]{1,0,2,3:T(2,128)(2,1)}, u32[]{:S(2)}, u32[]{:S(2)}) %all-to-all-start) | async-done | bytes 3145760 | tf_op jit(solution)/shard_map/all_to_all | solution.py:149
  250.6 55.7 %while.22 = (s32[]{:T(128)}, bf16[2,1024,256]{1,2,0:T(8,128)(2,1)S(1)}, f32[2,4,1024]{2,1,0:T(4,128)}, bf16[2,1024,3,256]{1,3,2,0:T(8,128)(2,1)}, s32[]{:T(128)}) while((s32[]{:T(128)}, bf16[2,1024,256]{1,2,0:T(8,128)(2,1)S(1)}, f32[2,4,1024]{2,1,0:T(4,128)}, bf16[2,1024,3,256]{1,3,2,0:T(8,128)(2,1)}, s32[]{:T(128)}) %tuple.80), condition=%wide.region_5.6_spmd, body=%wide.region_2.5_spmd.sunk | while | flops 1107554304 | bytes 59900484 | solution.py:49
  269.7 8.9 fusion.148
  312.0 9.0 all-gather.2
  345.4 10.3 fusion.87
  355.7 14.0 %fusion.79 = (f32[4096]{0:T(1024)}, bf16[512,4096]{1,0:T(8,128)(2,1)S(1)}) fusion(f32[512,4096]{1,0:T(8,128)} %fusion.87, f32[4096]{0:T(1024)S(1)} %bitcast.233, bf16[512,1024]{1,0:T(8,128)(2,1)} %bitcast.221, bf16[4096,1024]{1,0:T(8,128)(2,1)} %all-gather.19.cloned.1.call-done), kind=kOutput, calls=%fused_computation.133 | convolution fusion | flops 4341100544 | bytes 22052864 | tf_op jit(solution)/shard_map/dot_general | solution.py:176
  377.7 8.8 convolution_add_fusion.2
  394.9 11.6 fusion.57
  416.6 26.3 %all-to-all-done.2 = bf16[2,256,1024]{1,0,2:T(2,128)(2,1)S(1)} async-done(((bf16[2,256,1024]{1,0,2:T(2,128)(2,1)}), bf16[2,256,1024]{1,0,2:T(2,128)(2,1)S(1)}, u32[]{:S(2)}, u32[]{:S(2)}) %all-to-all-start.2) | async-done | bytes 1048608 | tf_op jit(solution)/shard_map/all_to_all | solution.py:197
  444.6 157.6 %while.23 = (s32[]{:T(128)}, bf16[2,1024,3,256]{1,3,2,0:T(8,128)(2,1)}, bf16[2,1024,3,256]{1,3,2,0:T(8,128)(2,1)}, f32[2,4,1024]{2,1,0:T(4,128)}, bf16[2,1024,256]{1,2,0:T(8,128)(2,1)S(1)}, /*index=5*/s32[]{:T(128)}) while((s32[]{:T(128)}, bf16[2,1024,3,256]{1,3,2,0:T(8,128)(2,1)}, bf16[2,1024,3,256]{1,3,2,0:T(8,128)(2,1)}, ...), condition=%wide.region_12.13_spmd, body=%wide.region_10.12_spmd.sunk | while | flops 2777950208 | bytes 133251664 | solution.py:198
  454.5 11.4 fusion.162
  466.6 27.4 %fusion.164 = bf16[4,64,1024]{2,1,0:T(8,128)(2,1)S(1)} fusion(bf16[1024,4,64]{0,2,1:T(8,128)(2,1)S(1)} %bitcast.193, f32[4,1024,1024]{1,2,0:T(8,128)} %fusion.162, f32[4,1024,1024]{1,2,0:T(8,128)} %fusion.160, f32[4,1024]{1,0:T(4,128)S(1)} %dynamic-slice_bitcast_fusion.8), kind=kOutput, calls=%fused_computation.23.clone.1 | convolution fusion | flops 574886912 | bytes 34619392 | tf_op jit(solution)/shard_map/while/body/eval_jaxpr/hqk,khd->qhd/dot_general | solution.py:74
  494.0 24.9 %fusion.163 = bf16[4,64,1024]{2,1,0:T(8,128)(2,1)S(1)} fusion(bf16[1024,4,64]{0,2,1:T(8,128)(2,1)S(1)} %bitcast.191, f32[4,1024,1024]{1,2,0:T(8,128)} %fusion.162, f32[4,1024,1024]{1,2,0:T(8,128)} %fusion.160, f32[4,1024]{1,0:T(4,128)S(1)} %dynamic-slice_bitcast_fusion.8), kind=kOutput, calls=%fused_computation.24.clone.1 | convolution fusion | flops 574886912 | bytes 34619392 | tf_op jit(solution)/shard_map/while/body/eval_jaxpr/hqk,qhd->khd/dot_general | solution.py:77
  546.8 23.9 %fusion.164 = bf16[4,64,1024]{2,1,0:T(8,128)(2,1)S(1)} fusion(bf16[1024,4,64]{0,2,1:T(8,128)(2,1)S(1)} %bitcast.193, f32[4,1024,1024]{1,2,0:T(8,128)} %fusion.162, f32[4,1024,1024]{1,2,0:T(8,128)} %fusion.160, f32[4,1024]{1,0:T(4,128)S(1)} %dynamic-slice_bitcast_fusion.8), kind=kOutput, calls=%fused_computation.23.clone.1 | convolution fusion | flops 574886912 | bytes 34619392 | tf_op jit(solution)/shard_map/while/body/eval_jaxpr/hqk,khd->qhd/dot_general | solution.py:74
  570.7 22.8 %fusion.163 = bf16[4,64,1024]{2,1,0:T(8,128)(2,1)S(1)} fusion(bf16[1024,4,64]{0,2,1:T(8,128)(2,1)S(1)} %bitcast.191, f32[4,1024,1024]{1,2,0:T(8,128)} %fusion.162, f32[4,1024,1024]{1,2,0:T(8,128)} %fusion.160, f32[4,1024]{1,0:T(4,128)S(1)} %dynamic-slice_bitcast_fusion.8), kind=kOutput, calls=%fused_computation.24.clone.1 | convolution fusion | flops 574886912 | bytes 34619392 | tf_op jit(solution)/shard_map/while/body/eval_jaxpr/hqk,qhd->khd/dot_general | solution.py:77
  609.8 74.1 %all_to_all.66 = bf16[2,1024,3,256]{3,0,2,1:T(2,128)(2,1)S(1)} all-to-all(bf16[2,1024,3,256]{3,0,2,1:T(2,128)(2,1)S(1)} %copy.100), channel_id=1, replica_groups=mesh['dp'=8,'seq'=4] {'seq'}, dimensions={1} | all-to-all | bytes 6291456 | tf_op jit(solution)/shard_map/all_to_all | solution.py:199
  690.4 10.2 fusion.88
  701.7 18.5 %fusion.78 = f32[4096,1024]{1,0:T(8,128)} fusion(bf16[512,1024]{1,0:T(8,128)(2,1)S(1)} %bitcast.222, f32[512,4096]{1,0:T(8,128)} %fusion.87, f32[4096]{0:T(1024)S(1)} %bitcast.235), kind=kOutput, calls=%fused_computation.132 | convolution fusion | flops 4315938816 | bytes 26230784 | tf_op jit(solution)/shard_map/dot_general | solution.py:175
  720.7 70.7 %reduce-scatter.8.cloned.1.call-done = f32[128,3072]{1,0:T(8,128)} async-done(((f32[1024,3072]{1,0:T(8,128)}), f32[128,3072]{1,0:T(8,128)}) %reduce-scatter.8.cloned.1.call-update) | async-done | bytes 1572880 | tf_op jit(solution)/shard_map/reduce_scatter | solution.py:242
  791.4 119.8 %reduce-scatter.14.cloned.1.call-done = f32[512,1024]{1,0:T(8,128)} async-done(((f32[4096,1024]{1,0:T(8,128)}), f32[512,1024]{1,0:T(8,128)}) %reduce-scatter.14.cloned.1.call-update) | async-done | bytes 2097168 | tf_op jit(solution)/shard_map/reduce_scatter | solution.py:248
  928.3 24.3 %psum.63 = f32[2,6144]{1,0:T(2,128)S(1)} all-reduce(f32[2,6144]{1,0:T(2,128)S(1)} %bitcast.232), channel_id=1, replica_groups=mesh['dp'=8,'seq'=4] {'seq'}, use_global_device_ids=true, to_apply=%region_21.22 | all-reduce | flops 12288 | bytes 98304 | tf_op jit(solution)/shard_map/psum | solution.py:219
  952.6 10.2 fusion.63
  974.8 24.4 %all-reduce.5 = (f32[6144]{0:T(1024)S(1)}, f32[2048]{0:T(1024)S(1)}, f32[1024]{0:T(1024)S(1)}, f32[4096]{0:T(1024)S(1)}, f32[1024]{0:T(1024)S(1)}) all-reduce(f32[6144]{0:T(1024)S(1)} %reduce_sum.244, f32[2048]{0:T(1024)S(1)} %pad_maximum_fusion, f32[1024]{0:T(1024)S(1)} %copy-done.31, ...), channel_id=3, replica_groups=mesh['dp'=8,'seq'=4] {'dp'}, use_global_device_ids=true, to_apply=%region_24.25.clone | all-reduce | flops 14336 | bytes 114688
  1000.2 12.2 all-reduce.6
  1024.7 113.7 %all-reduce.10.cloned.1.call-done = (f32[128,3072]{1,0:T(8,128)}, f32[128,1024]{1,0:T(8,128)}, f32[128,4096]{1,0:T(8,128)}, f32[512,1024]{1,0:T(8,128)}) async-done(((f32[128,3072]{1,0:T(8,128)}, f32[128,1024]{1,0:T(8,128)}, f32[128,4096]{1,0:T(8,128)}, f32[512,1024]{1,0:T(8,128)}), (f32[128,3072]{1,0:T(8,128)}, f32[128,1024]{1,0:T(8,128)}, f32[128,4096]{1,0:T(8,128)}, ...) | async-done | bytes 6291472 | tf_op jit(solution)/shard_map/psum | solution.py:251
  1138.3 159.5 %reduce-scatter.6.cloned.1.call-done = f32[128,6144]{1,0:T(8,128)} async-done(((f32[1024,6144]{1,0:T(8,128)}), f32[128,6144]{1,0:T(8,128)}) %reduce-scatter.6.cloned.1.call-update) | async-done | bytes 3145744 | tf_op jit(solution)/shard_map/reduce_scatter | solution.py:240
  (228 shorter events, 252.3 us)
Async XLA Ops:
  7.2 24.0 %copy-start = (bf16[2,256,1024]{2,1,0:T(8,128)(2,1)S(1)}, bf16[2,256,1024]{2,1,0:T(8,128)(2,1)}, u32[]{:S(2)}) copy-start(bf16[2,256,1024]{2,1,0:T(8,128)(2,1)} %param.17) | copy-start | bytes 3145732
  7.2 77.5 %copy-start.21 = (bf16[2,1024]{1,0:T(2,128)(2,1)S(1)}, bf16[2,1024]{1,0:T(2,128)(2,1)}, u32[]{:S(2)}) copy-start(bf16[2,1024]{1,0:T(2,128)(2,1)} %param.18) | copy-start | bytes 12292
  7.2 77.5 %all-gather.11.cloned.1.call-start = ((), (), s32[]{:S(2)}) async-start(), calls=%async_computation.9 | async-start | bytes 14155776 | tf_op jit(solution)/shard_map/all_gather | solution.py:121
  7.9 124.0 %all-gather.13.cloned.1.call-start = ((), (), s32[]{:S(2)}) async-start(), calls=%async_computation.10 | async-start | bytes 7077888 | tf_op jit(solution)/shard_map/all_gather | solution.py:123
  8.7 331.4 %all-gather.15.cloned.1.call-start = ((), (), s32[]{:S(2)}) async-start(), calls=%async_computation.11 | async-start | bytes 2359296 | tf_op jit(solution)/shard_map/all_gather | solution.py:125
  9.4 336.0 %all-gather.17.cloned.1.call-start = ((), (), s32[]{:S(2)}) async-start(), calls=%async_computation.12 | async-start | bytes 9437184 | tf_op jit(solution)/shard_map/all_gather | solution.py:127
  31.4 59.7 %copy-start.19 = (f32[2,256]{1,0:T(2,128)}, f32[2,256]{1,0:T(2,128)S(1)}, u32[]{:S(2)}) copy-start(f32[2,256]{1,0:T(2,128)S(1)} %broadcast_multiply_fusion.1) | copy-start | bytes 6148
  31.9 52.8 %copy-start.29 = (f32[2,256]{1,0:T(2,128)}, f32[2,256]{1,0:T(2,128)S(1)}, u32[]{:S(2)}) copy-start(f32[2,256]{1,0:T(2,128)S(1)} %fusion.53) | copy-start | bytes 6148
  31.9 59.3 %copy-start.25 = (f32[2,256]{1,0:T(2,128)}, f32[2,256]{1,0:T(2,128)S(1)}, u32[]{:S(2)}) copy-start(f32[2,256]{1,0:T(2,128)S(1)} %fusion.72) | copy-start | bytes 6148
  91.1 48.4 %copy-start.17 = (f32[2,1,1,1024]{3,0,1,2:T(2,128)}, f32[2,1,1,1024]{3,0,1,2:T(2,128)S(1)}, u32[]{:S(2)}) copy-start(f32[2,1,1,1024]{3,0,1,2:T(2,128)S(1)} %copy.125) | copy-start | bytes 24580
  91.6 47.9 %copy-start.15 = (bf16[2,256,1024]{2,1,0:T(8,128)(2,1)}, bf16[2,256,1024]{2,1,0:T(8,128)(2,1)S(1)}, u32[]{:S(2)}) copy-start(bf16[2,256,1024]{2,1,0:T(8,128)(2,1)S(1)} %fusion.51) | copy-start | bytes 3145732
  161.2 76.1 %all-to-all-start = ((bf16[2,256,3,1024]{1,0,2,3:T(2,128)(2,1)}), bf16[2,256,3,1024]{1,0,2,3:T(2,128)(2,1)}, u32[]{:S(2)}, u32[]{:S(2)}) async-start(bf16[2,256,3,1024]{1,0,2,3:T(2,128)(2,1)} %copy.91), calls=%async_computation | async-start | bytes 6291456 | tf_op jit(solution)/shard_map/all_to_all | solution.py:149
  165.9 189.8 %all-gather.19.cloned.1.call-start = ((), (), s32[]{:S(2)}) async-start(), calls=%async_computation.13 | async-start | bytes 9437184 | tf_op jit(solution)/shard_map/all_gather | solution.py:129
  306.3 14.6 %copy-start.36 = (bf16[512]{0:T(512)(128)(2,1)S(1)}, bf16[512]{0:T(512)(128)(2,1)}, u32[]{:S(2)}) copy-start(bf16[512]{0:T(512)(128)(2,1)} %param.26) | copy-start | bytes 3076
  306.3 22.6 %copy-start.38 = (bf16[128]{0:T(256)(128)(2,1)S(1)}, bf16[128]{0:T(256)(128)(2,1)}, u32[]{:S(2)}) copy-start(bf16[128]{0:T(256)(128)(2,1)} %param.28) | copy-start | bytes 772
  306.3 31.4 %copy-start.11 = (bf16[2,256,1024]{2,1,0:T(8,128)(2,1)S(1)}, bf16[2,256,1024]{2,1,0:T(8,128)(2,1)}, u32[]{:S(2)}) copy-start(bf16[2,256,1024]{2,1,0:T(8,128)(2,1)} %param.29) | copy-start | bytes 3145732
  308.4 30.6 %all-to-all-start.1 = ((bf16[2,1024,256]{2,0,1:T(2,128)(2,1)}), bf16[2,1024,256]{2,0,1:T(2,128)(2,1)S(1)}, u32[]{:S(2)}, u32[]{:S(2)}) async-start(bf16[2,1024,256]{2,0,1:T(2,128)(2,1)} %copy.95), calls=%async_computation.1 | async-start | bytes 2097152 | tf_op jit(solution)/shard_map/all_to_all | solution.py:151
  311.9 408.7 %reduce-scatter.10.cloned.1.call-start = ((), (), s32[]{:S(2)}) async-start(), calls=%async_computation.16 | async-start | bytes 4718592 | tf_op jit(solution)/shard_map/reduce_scatter | solution.py:244
  328.9 47.5 %copy-start.34 = (f32[8,1,512]{2,1,0:T(1,128)}, f32[8,1,512]{2,1,0:T(1,128)S(1)}, u32[]{:S(2)}) copy-start(f32[8,1,512]{2,1,0:T(1,128)S(1)} %convert_element_type.128) | copy-start | bytes 49156
  355.7 14.1 %copy-start.39 = (bf16[1024,4096]{1,0:T(8,128)(2,1)S(1)}, bf16[1024,4096]{1,0:T(8,128)(2,1)}, u32[]{:S(2)}) copy-start(bf16[1024,4096]{1,0:T(8,128)(2,1)} %all-gather.17.cloned.1.call-done) | copy-start | bytes 25165828
  394.9 325.8 %reduce-scatter.12.cloned.1.call-start = ((), (), s32[]{:S(2)}) async-start(), calls=%async_computation.17 | async-start | bytes 18874368 | tf_op jit(solution)/shard_map/reduce_scatter | solution.py:246
  411.6 31.3 %all-to-all-start.2 = ((bf16[2,256,1024]{1,0,2:T(2,128)(2,1)}), bf16[2,256,1024]{1,0,2:T(2,128)(2,1)S(1)}, u32[]{:S(2)}, u32[]{:S(2)}) async-start(bf16[2,256,1024]{1,0,2:T(2,128)(2,1)} %copy.97), calls=%async_computation.2 | async-start | bytes 2097152 | tf_op jit(solution)/shard_map/all_to_all | solution.py:197
  416.6 374.8 %reduce-scatter.8.cloned.1.call-start = ((), (), s32[]{:S(2)}) async-start(), calls=%async_computation.15 | async-start | bytes 14155776 | tf_op jit(solution)/shard_map/reduce_scatter | solution.py:242
  686.4 14.1 %copy-start.2 = (bf16[2,4,256,3,256]{4,1,3,2,0:T(4,128)(2,1)}, bf16[2,4,256,3,256]{4,1,3,2,0:T(4,128)(2,1)S(1)}, u32[]{:S(2)}) copy-start(bf16[2,4,256,3,256]{4,1,3,2,0:T(4,128)(2,1)S(1)} %copy.124) | copy-start | bytes 9437188
  700.5 210.6 %reduce-scatter.14.cloned.1.call-start = ((), (), s32[]{:S(2)}) async-start(), calls=%async_computation.18 | async-start | bytes 18874368 | tf_op jit(solution)/shard_map/reduce_scatter | solution.py:248
  720.3 418.0 %all-reduce.10.cloned.1.call-start = ((), (), s32[]{:S(2)}) async-start(), calls=%async_computation.19 | async-start | bytes 12582912 | tf_op jit(solution)/shard_map/psum | solution.py:251
  911.2 386.6 %reduce-scatter.6.cloned.1.call-start = ((), (), s32[]{:S(2)}) async-start(), calls=%async_computation.14 | async-start | bytes 28311552 | tf_op jit(solution)/shard_map/reduce_scatter | solution.py:240
  917.8 10.4 copy-start.23
  917.9 10.4 copy-start.27
  917.9 34.7 %copy-start.22 = (bf16[2,1024]{1,0:T(2,128)(2,1)S(1)}, bf16[2,1024]{1,0:T(2,128)(2,1)}, u32[]{:S(2)}) copy-start(bf16[2,1024]{1,0:T(2,128)(2,1)} %param.18) | copy-start | bytes 12292
  972.1 40.3 %copy-start.4 = (f32[2,256,1024]{2,1,0:T(8,128)S(1)}, f32[2,256,1024]{2,1,0:T(8,128)}, u32[]{:S(2)}) copy-start(f32[2,256,1024]{2,1,0:T(8,128)} %copy-done.3) | copy-start | bytes 6291460
  1138.3 164.2 %copy-start.14 = (f32[128,4096]{1,0:T(8,128)S(1)}, f32[128,4096]{1,0:T(8,128)}, u32[]{:S(2)}) copy-start(f32[128,4096]{1,0:T(8,128)} %get-tuple-element.297) | copy-start | bytes 6291460
  (24 other events, 118.4 us)
Sparse Core Ops, SparseCore 0:
  9.9 74.7 all-gather.10
  86.6 45.3 all-gather.12
  133.9 27.7 all-gather.14
  163.4 54.2 all-gather.16
  219.4 54.2 all-gather.18
  395.0 51.5 reduce-scatter.9
  450.1 116.1 reduce-scatter.11
  700.7 90.6 reduce-scatter.7
  794.9 116.1 reduce-scatter.13
  913.6 224.6 all-reduce.9
  1142.5 155.2 reduce-scatter.5
where the time goes:
time: 1320 us; the launch traced here: 1310 us
  waiting for transfers between devices  657 us (50%)
  matrix products  312 us (24%)
  blocking collectives  180 us (14%)
  local copies, waits for them, and re-layouts  87.8 us (7%)
  other arithmetic  43.1 us (3%)
  between operations  17.6 us (1%)
  starting transfers between devices  14 us (1%)
    reduce_scatter x1, waiting for transfers between devices, body(): lax.psum_scatter(ada_weight_local, 'dp', scatter_dimension=0, tiled=True)  159 us
    reduce_scatter x1, waiting for transfers between devices, body(): lax.psum_scatter(down_weight_grad, 'dp', scatter_dimension=0, tiled=True)  120 us
    psum x1, waiting for transfers between devices, body(): lax.psum((share_qkv, share_qv, share_out, share_out_bias, share_up, share...  114 us
    all_to_all x1, blocking collectives, body(): lax.all_to_all(grad_blocks, 'seq', split_axis=1, concat_axis=3, tiled=True)  74.1 us
    all_to_all x1, waiting for transfers between devices, body(): lax.all_to_all(projected, 'seq', split_axis=3, concat_axis=1, tiled=True)  70.8 us
    reduce_scatter x1, waiting for transfers between devices, body(): lax.psum_scatter(qkv_weight_grad, 'dp', scatter_dimension=0, tiled=True)  70.7 us
    all_gather x1, waiting for transfers between devices, body(): lax.all_gather(ada_weight, 'dp', axis=0, tiled=True)  52.8 us
    dot_general x2, matrix products, attend_grad(): jnp.einsum('hqk,khd->qhd', grad_scores, key_part, preferred_element_type=...  51.3 us
  transfers between devices with their start and end apart: 14, of which 8 were waited for; matrix products, arithmetic and copies ran while one was open for 30% of the time, Pallas kernels for 0%

commit v1 on v0

v1 whole, which is shorter than its diff:
```python
import functools

import jax
import jax.numpy as jnp
from jax import lax
from jax.experimental import pallas as pl
from jax.experimental.pallas import tpu as pltpu
from jax.sharding import PartitionSpec as P

HD = 64
LANES = 128
EPSILON = 1e-06
HALF = jnp.bfloat16
F32 = jnp.float32


def nn(a, b):
    return jnp.dot(a, b, preferred_element_type=F32)


def nt(a, b):
    return lax.dot_general(a, b, (((1,), (1,)), ((), ())), preferred_element_type=F32)


def tn(a, b):
    return lax.dot_general(a, b, (((0,), (0,)), ((), ())), preferred_element_type=F32)


def attend_kernel(groups, *refs):
    q_ref = refs[0]
    k_refs = refs[1 : 1 + groups]
    v_refs = refs[1 + groups : 1 + 2 * groups]
    out_ref, lse_ref, lse_acc = refs[1 + 2 * groups :]
    step = pl.program_id(0)
    rows = q_ref.shape[0]
    block = 256
    low = lax.broadcasted_iota(jnp.int32, (block, LANES), 1) < HD
    lane = lax.broadcasted_iota(jnp.int32, (block, LANES), 1)
    for start in range(0, rows, block):
        here = pl.ds(start, block)
        q = q_ref[here, :] * HALF(HD**-0.5)
        pieces = []
        for head in range(2):
            own = low if head == 0 else jnp.logical_not(low)
            qm = jnp.where(own, q, jnp.zeros_like(q))
            scores = [nt(qm, k[...]) for k in k_refs]
            peak = functools.reduce(
                jnp.maximum, [jnp.max(s, axis=-1, keepdims=True) for s in scores]
            )
            raised = [jnp.exp(s - peak) for s in scores]
            total = sum(jnp.sum(e, axis=-1, keepdims=True) for e in raised)
            mixed = sum(nn(e.astype(HALF), v[...]) for e, v in zip(raised, v_refs))
            pieces.append(mixed / total)
            spot = lane == 2 * step + head
            logsum = jnp.broadcast_to(peak + jnp.log(total), (block, LANES))
            lse_acc[here, :] = jnp.where(spot, logsum, lse_acc[here, :])
        out_ref[here, :] = jnp.where(low, pieces[0], pieces[1]).astype(HALF)

    @pl.when(step == pl.num_programs(0) - 1)
    def _():
        lse_ref[...] = lse_acc[...].T


def attend(projected, others, width):
    rows = projected.shape[0]
    groups = 1 + len(others)
    tiles = width // LANES
    col = lambda base: pl.BlockSpec((rows, LANES), lambda i, base=base: (0, base + i))
    return pl.pallas_call(
        functools.partial(attend_kernel, groups),
        grid=(tiles,),
        out_shape=(
            jax.ShapeDtypeStruct((rows, width), HALF),
            jax.ShapeDtypeStruct((LANES, rows), F32),
        ),
        in_specs=[col(0), col(tiles)] + [col(0)] * len(others) + [col(2 * tiles)] + [col(tiles)] * len(others),
        out_specs=(col(0), pl.BlockSpec((LANES, rows), lambda i: (0, 0))),
        scratch_shapes=[pltpu.VMEM((rows, LANES), F32)],
        compiler_params=pltpu.CompilerParams(vmem_limit_bytes=48 << 20),
        name="attend",
    )(projected, projected, *others, projected, *others)


def attend_grad_kernel(groups, *refs):
    q_ref = refs[0]
    k_refs = refs[1 : 1 + groups]
    v_refs = refs[1 + groups : 1 + 2 * groups]
    do_ref, o_ref, lse_ref = refs[1 + 2 * groups : 4 + 2 * groups]
    dq_ref = refs[4 + 2 * groups]
    dk_refs = refs[5 + 2 * groups : 5 + 3 * groups]
    dv_refs = refs[5 + 3 * groups : 5 + 4 * groups]
    step = pl.program_id(0)
    rows = q_ref.shape[0]
    block = 256
    scale = HALF(HD**-0.5)
    q = q_ref[...] * scale
    grad = do_ref[...]
    product = grad.astype(F32) * o_ref[...].astype(F32)
    top = product.astype(HALF)
    rest = (product - top.astype(F32)).astype(HALF)
    pick = lax.broadcasted_iota(jnp.int32, (8, LANES), 0) == (
        lax.broadcasted_iota(jnp.int32, (8, LANES), 1) // HD
    )
    pick = jnp.where(pick, 1.0, 0.0).astype(HALF)
    inner = nt(pick, top) + nt(pick, rest)
    low = lax.broadcasted_iota(jnp.int32, (block, LANES), 1) < HD
    dq_t = [jnp.zeros((LANES, rows), F32) for _ in range(2)]
    for k_ref, v_ref, dk_ref, dv_ref in zip(k_refs, v_refs, dk_refs, dv_refs):
        for start in range(0, rows, block):
            here = pl.ds(start, block)
            k = k_ref[here, :]
            v = v_ref[here, :]
            k_t = k.T
            dks, dvs = [], []
            for head in range(2):
                own = low if head == 0 else jnp.logical_not(low)
                lse = lse_ref[pl.ds(2 * step + head, 1), :]
                scores = nt(jnp.where(own, k, jnp.zeros_like(k)), q)
                probs = jnp.exp(scores - lse)
                dvs.append(nn(probs.astype(HALF), grad))
                gp = nt(jnp.where(own, v, jnp.zeros_like(v)), grad)
                gs = (probs * (gp - inner[head : head + 1, :])).astype(HALF)
                dks.append(nn(gs, q))
                dq_t[head] = dq_t[head] + nn(k_t, gs)
            dk_ref[here, :] = jnp.where(low, dks[0], dks[1]).astype(HALF)
            dv_ref[here, :] = jnp.where(low, dvs[0], dvs[1]).astype(HALF)
    upper = lax.broadcasted_iota(jnp.int32, (LANES, rows), 0) < HD
    dq = jnp.where(upper, dq_t[0], dq_t[1]).T * HD**-0.5
    dq_ref[...] = dq.astype(HALF)


def attend_grad(projected, others, grad, attended, logsum, width):
    rows = projected.shape[0]
    groups = 1 + len(others)
    tiles = width // LANES
    col = lambda base: pl.BlockSpec((rows, LANES), lambda i, base=base: (0, base + i))
    out = jax.ShapeDtypeStruct((rows, width), HALF)
    return pl.pallas_call(
        functools.partial(attend_grad_kernel, groups),
        grid=(tiles,),
        out_shape=(out,) * (1 + 2 * groups),
        in_specs=[col(0), col(tiles)]
        + [col(0)] * len(others)
        + [col(2 * tiles)]
        + [col(tiles)] * len(others)
        + [col(0), col(0), pl.BlockSpec((LANES, rows), lambda i: (0, 0))],
        out_specs=(col(0),) * (1 + 2 * groups),
        compiler_params=pltpu.CompilerParams(vmem_limit_bytes=48 << 20),
        name="attend_grad",
    )(projected, projected, *others, projected, *others, grad, attended, logsum)


def norm_parts(rows):
    centred = rows - jnp.mean(rows, axis=-1, keepdims=True)
    variance = jnp.mean(centred * centred, axis=-1, keepdims=True)
    inverse = lax.rsqrt(variance + EPSILON)
    return centred * inverse, inverse


def norm_grad(grad, hat, inverse, scale):
    g = grad * (1.0 + scale)
    return (
        g
        - jnp.mean(g, axis=-1, keepdims=True)
        - hat * jnp.mean(g * hat, axis=-1, keepdims=True)
    ) * inverse


def gelu_tanh(inputs):
    return jax.nn.gelu(inputs, approximate=True)


def body(
    tokens,
    condition,
    ada_weight,
    ada_bias,
    qkv_weight,
    qv_bias,
    out_weight,
    out_bias,
    up_weight,
    up_bias,
    down_weight,
    down_bias,
    cotangent,
):
    lats, part, width = tokens.shape
    dp = lax.axis_size("dp")
    seq = lax.axis_size("seq")
    me = lax.axis_index("dp")
    z = lax.axis_index("seq")
    core = me % 2
    pair = me // 2
    chip_lats = 2 * lats
    sub = seq // chip_lats
    first = core == 0

    def flip(x):
        return lax.ppermute(x, "dp", [(i, i ^ 1) for i in range(dp)])

    def shift(x, by):
        if by % sub == 0:
            return x
        return lax.ppermute(
            x, "seq", [(i, i // sub * sub + (i - by) % sub) for i in range(seq)]
        )

    def spread(x):
        halves = x.reshape(lats, 2, part // 2, width)
        keep = lax.dynamic_index_in_dim(halves, core, 1, keepdims=False)
        give = lax.dynamic_index_in_dim(halves, 1 - core, 1, keepdims=False)
        got = flip(give)
        both = jnp.concatenate(
            [jnp.where(first, keep, got), jnp.where(first, got, keep)], axis=0
        )
        both = both.reshape(seq, part // (2 * sub), width)
        return lax.all_to_all(both, "seq", 0, 0, tiled=True).reshape(-1, width)

    def collect(x):
        both = x.reshape(seq, part // (2 * sub), width)
        both = lax.all_to_all(both, "seq", 0, 0, tiled=True)
        both = both.reshape(2, lats, part // 2, width)
        mine = lax.dynamic_index_in_dim(both, core, 0, keepdims=False)
        give = lax.dynamic_index_in_dim(both, 1 - core, 0, keepdims=False)
        got = flip(give)
        return jnp.stack(
            [jnp.where(first, mine, got), jnp.where(first, got, mine)], axis=1
        ).reshape(lats, part, width)

    small = jnp.concatenate(
        [ada_bias, qv_bias, out_bias, up_bias, down_bias, condition.reshape(-1)]
    )
    small_all = lax.all_gather(small, "dp", axis=0, tiled=False)
    sizes = [a.shape[0] for a in (ada_bias, qv_bias, out_bias, up_bias, down_bias)]
    cuts = [0]
    for size in sizes:
        cuts.append(cuts[-1] + size)
    ada_bias_full, qv_full, out_bias_full, up_bias_full, down_bias_full = [
        small_all[:, a:b].reshape(-1).astype(F32) for a, b in zip(cuts[:-1], cuts[1:])
    ]
    cond_all = small_all[:, cuts[-1] :].reshape(dp * lats, width).astype(F32)
    depth = ada_weight.shape[0]
    silu_all = jax.nn.silu(cond_all).astype(HALF)
    silu_mine = lax.dynamic_slice_in_dim(silu_all, me * depth, depth, axis=1)
    partial = nn(silu_mine, ada_weight)
    row_here = z // sub
    wanted = partial.reshape(dp // 2, chip_lats, 6 * width)
    wanted = lax.dynamic_index_in_dim(wanted, row_here, 1, keepdims=True)
    wanted = jnp.broadcast_to(wanted, (dp // 2, 2, 6 * width)).reshape(dp, 6 * width)
    modulation = lax.psum_scatter(wanted, "dp", scatter_dimension=0, tiled=True)[0]
    modulation = (modulation + ada_bias_full).reshape(6, 1, width)
    shift_a, scale_a, gate_a, shift_b, scale_b, gate_b = [modulation[i] for i in range(6)]

    qkv_full = lax.all_gather(qkv_weight, "dp", axis=0, tiled=True)
    out_full = lax.all_gather(out_weight, "dp", axis=0, tiled=True)
    up_full = lax.all_gather(up_weight, "dp", axis=0, tiled=True)
    down_full = lax.all_gather(down_weight, "dp", axis=0, tiled=True)

    rows = spread(tokens).astype(F32)
    cot = spread(cotangent).astype(F32)

    hat_a, inverse_a = norm_parts(rows)
    normed_a = (hat_a * (1.0 + scale_a) + shift_a).astype(HALF)
    bias_all = jnp.concatenate([qv_full[:width], jnp.zeros((width,), F32), qv_full[width:]])
    projected = (nn(normed_a, qkv_full) + bias_all).astype(HALF)
    kv = projected[:, width:]
    ways = [(a, s) for s in range(sub) for a in range(2)]
    others = [shift(flip(kv) if a else kv, s) for a, s in ways[1:]]
    attended, logsum = attend(projected, others, width)
    branch_a = nn(attended, out_full) + out_bias_full
    middle = rows + gate_a * branch_a
    hat_b, inverse_b = norm_parts(middle)
    normed_b = (hat_b * (1.0 + scale_b) + shift_b).astype(HALF)
    hidden_pre = nn(normed_b, up_full) + up_bias_full
    hidden = gelu_tanh(hidden_pre).astype(HALF)
    branch_b = nn(hidden, down_full) + down_bias_full
    output = collect((middle + gate_b * branch_b).astype(HALF))

    grad_gate_b = jnp.sum(cot * branch_b, axis=0)
    grad_branch_b = cot * gate_b
    down_bias_grad = jnp.sum(grad_branch_b, axis=0)
    grad_branch_half = grad_branch_b.astype(HALF)
    down_weight_grad = tn(hidden, grad_branch_half).astype(HALF)
    grad_hidden = nt(grad_branch_half, down_full)
    _, gelu_back = jax.vjp(gelu_tanh, hidden_pre)
    grad_pre = gelu_back(grad_hidden)[0]
    up_bias_grad = jnp.sum(grad_pre, axis=0)
    grad_pre_half = grad_pre.astype(HALF)
    up_weight_grad = tn(normed_b, grad_pre_half).astype(HALF)
    grad_normed_b = nt(grad_pre_half, up_full)
    grad_shift_b = jnp.sum(grad_normed_b, axis=0)
    grad_scale_b = jnp.sum(grad_normed_b * hat_b, axis=0)
    grad_middle = cot + norm_grad(grad_normed_b, hat_b, inverse_b, scale_b)
    grad_gate_a = jnp.sum(grad_middle * branch_a, axis=0)
    grad_branch_a = grad_middle * gate_a
    out_bias_grad = jnp.sum(grad_branch_a, axis=0)
    grad_branch_a_half = grad_branch_a.astype(HALF)
    out_weight_grad = tn(attended, grad_branch_a_half).astype(HALF)
    grad_attended = nt(grad_branch_a_half, out_full).astype(HALF)

    results = attend_grad(projected, others, grad_attended, attended, logsum, width)
    count = len(ways)
    grad_query = results[0]
    grad_keys = results[1 : 1 + count]
    grad_values = results[1 + count :]
    grad_kv = [jnp.concatenate([k, v], axis=1) for k, v in zip(grad_keys, grad_values)]
    total_kv = grad_kv[0].astype(F32)
    for (a, s), part_kv in zip(ways[1:], grad_kv[1:]):
        back = shift(part_kv, -s)
        total_kv = total_kv + (flip(back) if a else back).astype(F32)
    grad_projected = jnp.concatenate([grad_query, total_kv.astype(HALF)], axis=1)
    qkv_weight_grad = tn(normed_a, grad_projected).astype(HALF)
    grad_proj_float = grad_projected.astype(F32)
    qv_bias_grad = jnp.concatenate(
        [
            jnp.sum(grad_proj_float[:, :width], axis=0),
            jnp.sum(grad_proj_float[:, 2 * width :], axis=0),
        ]
    )
    grad_normed_a = nt(grad_projected, qkv_full)
    grad_shift_a = jnp.sum(grad_normed_a, axis=0)
    grad_scale_a = jnp.sum(grad_normed_a * hat_a, axis=0)
    grad_tokens = grad_middle + norm_grad(grad_normed_a, hat_a, inverse_a, scale_a)
    tokens_grad = collect(grad_tokens.astype(HALF)).astype(F32)

    grad_mod = jnp.concatenate(
        [grad_shift_a, grad_scale_a, grad_gate_a, grad_shift_b, grad_scale_b, grad_gate_b]
    )
    every = lax.all_gather(grad_mod, "seq", axis=0, tiled=False)
    every = lax.all_gather(every, "dp", axis=0, tiled=False)
    every = every.reshape(dp // 2, 2, chip_lats, sub, 6 * width).sum(axis=(1, 3))
    every = every.reshape(dp * lats, 6 * width)
    every_half = every.astype(HALF)
    ada_weight_grad = tn(silu_mine, every_half)
    bias_len = ada_bias.shape[0]
    ada_bias_grad = jnp.sum(
        lax.dynamic_slice_in_dim(every, me * bias_len, bias_len, axis=1), axis=0
    )
    cond_part = nt(every_half, ada_weight).reshape(dp, lats, depth)
    cond_part = lax.all_to_all(cond_part, "dp", 0, 0, tiled=True)
    cond_part = cond_part.transpose(1, 0, 2).reshape(lats, width)
    cond_float = condition.astype(F32)
    sigmoid_cond = jax.nn.sigmoid(cond_float)
    silu_slope = sigmoid_cond * (1.0 + cond_float * (1.0 - sigmoid_cond))
    condition_grad = silu_slope * cond_part

    def reduce_weight(grad):
        share = lax.psum_scatter(grad, "dp", scatter_dimension=0, tiled=True)
        return lax.psum(share, "seq").astype(F32)

    bias_parts = jnp.concatenate(
        [
            b.reshape(dp, -1)
            for b in (qv_bias_grad, out_bias_grad, up_bias_grad, down_bias_grad)
        ],
        axis=1,
    )
    bias_parts = lax.psum_scatter(bias_parts, "dp", scatter_dimension=0, tiled=True)
    bias_parts = lax.psum(bias_parts, "seq")[0]
    cuts = [c - sizes[0] for c in cuts[1:]]
    qv_g, ob_g, ub_g, db_g = [bias_parts[a:b] for a, b in zip(cuts[:-1], cuts[1:])]
    return (
        output,
        tokens_grad,
        condition_grad,
        ada_weight_grad,
        ada_bias_grad,
        reduce_weight(qkv_weight_grad),
        qv_g,
        reduce_weight(out_weight_grad),
        ob_g,
        reduce_weight(up_weight_grad),
        ub_g,
        reduce_weight(down_weight_grad),
        db_g,
    )


def solution(mesh):
    return jax.shard_map(
        body,
        mesh=mesh,
        in_specs=(
            P("dp", "seq", None),
            P("dp", None),
            P("dp", None),
            P("dp"),
            P("dp", None),
            P("dp"),
            P("dp", None),
            P("dp"),
            P("dp", None),
            P("dp"),
            P("dp", None),
            P("dp"),
            P("dp", "seq", None),
        ),
        out_specs=(
            P("dp", "seq", None),
            P("dp", "seq", None),
            P("dp", None),
            P("dp", None),
            P("dp"),
            P("dp", None),
            P("dp"),
            P("dp", None),
            P("dp"),
            P("dp", None),
            P("dp"),
            P("dp", None),
            P("dp"),
        ),
        check_vma=False,
    )
```

time: 1320 us -> 747 us (0.57)
  waiting for transfers between devices: 657 us -> 396 us
  matrix products: 312 us -> 104 us
  blocking collectives: 180 us -> 91.7 us
  local copies, waits for them, and re-layouts: 87.8 us -> 24.8 us
  Pallas kernels: 0 us -> 54.8 us
  other arithmetic: 43.1 us -> 29.1 us
    reduce_scatter x5 -> x4, waiting for transfers between devices: 350 us -> 141 us  [reduce_weight(): share = lax.psum_scatter(grad, 'dp', scatter_dimension=0, tiled=True)]
    dot_general x29 -> x15, matrix products: 312 us -> 104 us  [the longest x5 35.3 us: nt(): lax.dot_general(a, b, (((1,), (1,)), ((), ())), preferred_element_type=F32)]
    all_to_all x1 -> x0, blocking collectives: 74.1 us -> none  [body(): lax.all_to_all(grad_blocks, 'seq', split_axis=1, concat_axis=3, tiled=True)]
    psum x1, waiting for transfers between devices: 114 us -> 54.8 us  [reduce_weight(): return lax.psum(share, 'seq').astype(F32)]
    pallas_call x0 -> x2, Pallas kernels: none -> 54.8 us  [the longest x1 36 us: attend_grad(): pl.pallas_call(functools.partial(attend_grad_kernel, groups), grid=(tiles...]
    all_to_all x3 -> x5, waiting for transfers between devices: 97.1 us -> 51.5 us  [the longest x2 26.1 us: spread(): return lax.all_to_all(both, 'seq', 0, 0, tiled=True).reshape(-1, width)]
    unnamed x11, waiting for transfers between devices: 3.04 us -> 43.2 us
    reshape x5 -> x4, local copies, waits for them, and re-layouts: 27.7 us -> 1.06 us  [the longest x1 0.81 us: body(): jnp.broadcast_to(wanted, (dp // 2, 2, 6 * width)).reshape(dp, 6 * width)]
  transfers between devices with their start and end apart: 14 -> 21, of which waited for: 8 -> 12; matrix products, arithmetic and copies ran while one was open for 30% -> 14% of each run, Pallas kernels for 0% -> 3%
where the time goes in v1:
time: 747 us; the launch traced here: 740 us
  waiting for transfers between devices  396 us (53%)
  matrix products  104 us (14%)
  blocking collectives  91.7 us (12%)
  Pallas kernels  54.8 us (7%)
  other arithmetic  29.1 us (4%)
  local copies, waits for them, and re-layouts  24.8 us (3%)
  starting transfers between devices  24.1 us (3%)
  between operations  15.3 us (2%)
    reduce_scatter x4, waiting for transfers between devices, reduce_weight(): share = lax.psum_scatter(grad, 'dp', scatter_dimension=0, tiled=True)  141 us
    psum x1, waiting for transfers between devices, reduce_weight(): return lax.psum(share, 'seq').astype(F32)  54.8 us
    all_gather x1, waiting for transfers between devices, body(): down_full = lax.all_gather(down_weight, 'dp', axis=0, tiled=True)  43.9 us
    unnamed x11, waiting for transfers between devices  43.2 us
    all_gather x1, waiting for transfers between devices, body(): qkv_full = lax.all_gather(qkv_weight, 'dp', axis=0, tiled=True)  43 us
    pallas_call x1, Pallas kernels, attend_grad(): pl.pallas_call(functools.partial(attend_grad_kernel, groups), grid=(tiles...  36 us
    dot_general x5, matrix products, nt(): lax.dot_general(a, b, (((1,), (1,)), ((), ())), preferred_element_type=F32)  35.3 us
    dot_general x5, matrix products, tn(): lax.dot_general(a, b, (((0,), (0,)), ((), ())), preferred_element_type=F32)  34.7 us
  transfers between devices with their start and end apart: 21, of which 12 were waited for; matrix products, arithmetic and copies ran while one was open for 14% of the time, Pallas kernels for 3%

profile of v1, /device:TPU:0, one launch (start us, length us, event | category | flops | bytes accessed | tf_op | source)
XLA Modules:
  0.0 739.6 jit_solution(14201400726880329401)
XLA Ops:
  12.5 10.7 %all-gather.3 = bf16[8,1,3840]{2,1,0:T(2,128)(2,1)S(1)} all-gather(bf16[1,1,3840]{2,1,0:T(2,128)(2,1)S(1)} %reshape.243), channel_id=2, replica_groups=mesh['dp'=8,'seq'=4] {'dp'}, dimensions={0}, use_global_device_ids=true | all-gather | bytes 69120 | tf_op jit(solution)/shard_map/all_gather | solution.py:234
  32.8 4.9 all-to-all-start
  38.3 40.6 %all-reduce.6.cloned.1.call-done = f32[8,6144]{1,0:T(8,128)} async-done(((f32[8,6144]{1,0:T(8,128)}), f32[8,6144]{1,0:T(8,128)}) %all-reduce.6.cloned.1.call-update) | async-done | bytes 196624
  82.7 43.0 %all-gather.10.cloned.1.call-done = bf16[1024,3072]{1,0:T(8,128)(2,1)} async-done(((bf16[128,3072]{1,0:T(8,128)(2,1)}), bf16[1024,3072]{1,0:T(8,128)(2,1)}) %all-gather.10.cloned.1.call-update) | async-done | bytes 6291472 | tf_op jit(solution)/shard_map/all_gather | solution.py:255
  125.7 6.5 add_convert_fusion.refs_0_.refs_1_.refs_3_
  137.0 4.6 all-to-all-start.2
  141.7 26.1 %all-to-all-done.2 = bf16[4,128,1024]{2,1,0:T(8,128)(2,1)S(1)} async-done(((bf16[4,128,1024]{2,1,0:T(8,128)(2,1)}), bf16[4,128,1024]{2,1,0:T(8,128)(2,1)S(1)}, u32[]{:S(2)}, u32[]{:S(2)}) %all-to-all-start.2) | async-done | bytes 1048608 | tf_op jit(solution)/shard_map/all_to_all | solution.py:218
  169.1 18.8 %attend.1 = (bf16[512,1024]{1,0:T(8,128)(2,1)S(1)}, f32[128,512]{1,0:T(8,128)S(1)}) custom-call(bf16[512,3072]{1,0:T(8,128)(2,1)} %copy-done.5, bf16[512,3072]{1,0:T(8,128)(2,1)} %copy-done.5, bf16[512,2048]{1,0:T(8,128)(2,1)} %collective-permute-done.1.refs_2_.refs_4_, bf16[512,3072]{1,0:T(8,128)(2,1)} %copy-done.5, ...), custom_call_target="tpu_custom_call" | custom-call | tf_op jit(solution)/shard_map/attend/pallas_call | solution.py:69
  188.0 4.9 fusion.54
  194.5 16.9 %all-gather.14.cloned.1.call-done = bf16[1024,4096]{1,0:T(8,128)(2,1)} async-done(((bf16[128,4096]{1,0:T(8,128)(2,1)}), bf16[1024,4096]{1,0:T(8,128)(2,1)}) %all-gather.14.cloned.1.call-update) | async-done | bytes 8388624 | tf_op jit(solution)/shard_map/all_gather | solution.py:257
  211.4 12.1 %fusion.50 = f32[512,4096]{1,0:T(8,128)} fusion(bf16[1024,4096]{1,0:T(8,128)(2,1)} %all-gather.14.cloned.1.call-done, f32[512,1024]{1,0:T(8,128)} %copy-done.13, f32[1024]{0:T(1024)S(1)} %get-tuple-element.64, f32[1024]{0:T(1024)S(1)} %get-tuple-element.65, f32[512]{0:T(512)S(1)} %add_rsqrt_fusion, f32[512]{0:T(512)S(1)} %broadcast_multiply_fusion.4), kind=kOutput, calls=%fused_computation.138 | convolution fusion | flops 4297588736 | bytes 18886656 | tf_op jit(solution)/shard_map/dot_general | solution.py:18
  223.6 43.9 %all-gather.16.cloned.1.call-done = bf16[4096,1024]{1,0:T(8,128)(2,1)} async-done(((bf16[512,1024]{1,0:T(8,128)(2,1)}), bf16[4096,1024]{1,0:T(8,128)(2,1)}) %all-gather.16.cloned.1.call-update) | async-done | bytes 8388624 | tf_op jit(solution)/shard_map/all_gather | solution.py:258
  267.4 15.6 %fusion.52 = (f32[4096]{0:T(1024)S(1)}, bf16[512,4096]{1,0:T(8,128)(2,1)}) fusion(f32[512,4096]{1,0:T(8,128)} %fusion.50, f32[4096]{0:T(1024)S(1)} %bitcast.170, bf16[512,1024]{1,0:T(8,128)(2,1)S(1)} %copy-done.18, bf16[4096,1024]{1,0:T(8,128)(2,1)} %all-gather.16.cloned.1.call-done), kind=kOutput, calls=%fused_computation.140 | convolution fusion | flops 4341100544 | bytes 22052864 | tf_op jit(solution)/shard_map/dot_general | solution.py:22
  283.1 9.1 %multiply_reduce_fusion = (f32[1024]{0:T(1024)S(1)}, f32[512]{0:T(512)S(1)}, f32[512]{0:T(512)S(1)}, f32[1024]{0:T(1024)S(1)}, f32[512,1024]{1,0:T(8,128)S(1)}) fusion(f32[512,1024]{1,0:T(8,128)S(1)} %copy-done.14, f32[512]{0:T(512)S(1)} %add_rsqrt_fusion, f32[512]{0:T(512)S(1)} %broadcast_multiply_fusion.4, f32[1024]{0:T(1024)S(1)} %get-tuple-element.65, ...), kind=kOutput, calls=%fused_computation.44 | convolution fusion | flops 4299682816 | bytes 16797696 | tf_op jit(solution)/shard_map/dot_general | solution.py:22
  292.2 10.1 %fusion.8 = (f32[1024]{0:T(1024)S(1)}, bf16[512,1024]{1,0:T(8,128)(2,1)}, f32[1024]{0:T(1024)S(1)}, f32[1024]{0:T(1024)S(1)}, f32[512,1024]{1,0:T(8,128)S(1)}) fusion(bf16[4,128,1024]{2,1,0:T(8,128)(2,1)S(1)} %copy-done.9, f32[1024]{0:T(1024)S(1)} %get-tuple-element.61, f32[512,1024]{1,0:T(8,128)S(1)} %copy-done.14, f32[1024]{0:T(1024)S(1)} %get-tuple-element.63, ...), kind=kOutput, calls=%fused_computation.24 | convolution fusion | flops 4326421504 | bytes 27320320 | tf_op jit(solution)/shard_map/dot_general | solution.py:18
  304.6 36.0 %attend_grad.1 = (bf16[512,1024]{1,0:T(8,128)(2,1)S(1)}, bf16[512,1024]{1,0:T(8,128)(2,1)S(1)}, bf16[512,1024]{1,0:T(8,128)(2,1)S(1)}, bf16[512,1024]{1,0:T(8,128)(2,1)S(1)}, bf16[512,1024]{1,0:T(8,128)(2,1)S(1)}) custom-call(bf16[512,3072]{1,0:T(8,128)(2,1)} %copy-done.5, bf16[512,3072]{1,0:T(8,128)(2,1)} %copy-done.5, ...), custom_call_target="tpu_custom_call" | custom-call | tf_op jit(solution)/shard_map/attend_grad/pallas_call | solution.py:138
  347.1 3.0 add_convert_fusion.1
  351.5 5.6 convolution_convert_fusion.2
  357.1 10.9 %convolution_convert_fusion.1 = bf16[1024,4096]{1,0:T(8,128)(2,1)} fusion(bf16[512,4096]{1,0:T(8,128)(2,1)} %get-tuple-element.44, f32[512,1024]{1,0:T(8,128)} %copy-done.13, f32[1024]{0:T(1024)S(1)} %get-tuple-element.64, f32[1024]{0:T(1024)S(1)} %get-tuple-element.65, f32[512]{0:T(512)S(1)} %add_rsqrt_fusion, f32[512]{0:T(512)S(1)} %broadcast_multiply_fusion.4), kind=kOutput, calls=%fused_computation.10 | convolution fusion | flops 4301783040 | bytes 14692352 | tf_op jit(solution)/shard_map/dot_general | solution.py:26
  368.3 13.3 %convolution_convert_fusion = bf16[4096,1024]{1,0:T(8,128)(2,1)} fusion(bf16[512,1024]{1,0:T(8,128)(2,1)} %fusion.7, f32[512,4096]{1,0:T(8,128)} %fusion.50, f32[4096]{0:T(1024)S(1)} %bitcast.172), kind=kOutput, calls=%fused_computation.9 | convolution fusion | flops 4320133120 | bytes 17842176 | tf_op jit(solution)/shard_map/dot_general | solution.py:26
  381.7 4.6 all-to-all-start.1
  387.8 24.8 %all-to-all-done.1 = bf16[4,128,1024]{2,1,0:T(8,128)(2,1)} async-done(((bf16[4,128,1024]{2,1,0:T(8,128)(2,1)}), bf16[4,128,1024]{2,1,0:T(8,128)(2,1)}, u32[]{:S(2)}, u32[]{:S(2)}) %all-to-all-start.1) | async-done | bytes 1048608 | tf_op jit(solution)/shard_map/all_to_all | solution.py:222
  414.5 7.8 %fusion.23 = (f32[1024]{0:T(1024)S(1)}, f32[512]{0:T(512)S(1)}, f32[512]{0:T(512)S(1)}, f32[1024]{0:T(1024)S(1)}, f32[512,1024]{1,0:T(8,128)S(1)}) fusion(bf16[4,128,1024]{2,1,0:T(8,128)(2,1)} %copy-done.6, f32[512]{0:T(512)S(1)} %rsqrt_bitcast_fusion, f32[512]{0:T(512)S(1)} %get-tuple-element.73, f32[1024]{0:T(1024)S(1)} %get-tuple-element.67, ...), kind=kOutput, calls=%fused_computation.43 | convolution fusion | flops 3232756736 | bytes 12603392 | tf_op jit(solution)/shard_map/dot_general | solution.py:22
  424.0 4.3 all-to-all-start.3
  428.4 32.9 %all-gather.1 = f32[24576]{0:T(1024)S(1)} all-gather(f32[6144]{0:T(1024)S(1)} %constant_dynamic-update-slice_fusion), channel_id=3, replica_groups=mesh['dp'=8,'seq'=4] {'seq'}, dimensions={0}, use_global_device_ids=true | all-gather | bytes 122880 | tf_op jit(solution)/shard_map/all_gather | solution.py:330
  461.4 65.5 %reduce-scatter.9.cloned.1.call-done = bf16[128,4096]{1,0:T(8,128)(2,1)} async-done(((bf16[1024,4096]{1,0:T(8,128)(2,1)}), bf16[128,4096]{1,0:T(8,128)(2,1)}) %reduce-scatter.9.cloned.1.call-update) | async-done | bytes 1048592 | tf_op jit(solution)/shard_map/reduce_scatter | solution.py:349
  526.9 75.0 %reduce-scatter.11.cloned.1.call-done = bf16[512,1024]{1,0:T(8,128)(2,1)} async-done(((bf16[4096,1024]{1,0:T(8,128)(2,1)}), bf16[512,1024]{1,0:T(8,128)(2,1)}) %reduce-scatter.11.cloned.1.call-update) | async-done | bytes 1048592 | tf_op jit(solution)/shard_map/reduce_scatter | solution.py:349
  601.9 10.7 %all-gather.4 = f32[8,4,6144]{2,1,0:T(4,128)S(1)} all-gather(f32[1,4,6144]{2,1,0:T(4,128)S(1)} %reshape.245), channel_id=4, replica_groups=mesh['dp'=8,'seq'=4] {'dp'}, dimensions={0}, use_global_device_ids=true | all-gather | bytes 884736 | tf_op jit(solution)/shard_map/all_gather | solution.py:331
  615.6 25.2 %all-reduce.1 = f32[8,1024]{1,0:T(8,128)S(1)} all-reduce(f32[8,1024]{1,0:T(8,128)S(1)} %pad_maximum_fusion.7), channel_id=7, replica_groups=mesh['dp'=8,'seq'=4] {'dp'}, use_global_device_ids=true, to_apply=%region_24.25.clone | all-reduce | flops 8192 | bytes 65536
  641.5 12.3 %psum.36 = f32[1,1024]{1,0:T(1,128)S(1)} all-reduce(f32[1,1024]{1,0:T(1,128)S(1)} %constant_dynamic-slice_fusion.1), channel_id=1, replica_groups=mesh['dp'=8,'seq'=4] {'seq'}, use_global_device_ids=true, to_apply=%region_25.26 | all-reduce | flops 1024 | bytes 8192 | tf_op jit(solution)/shard_map/psum | solution.py:360
  659.6 3.3 all-to-all-start.4
  670.9 54.8 %all-reduce.8.cloned.1.call-done = (bf16[128,3072]{1,0:T(8,128)(2,1)}, bf16[128,1024]{1,0:T(8,128)(2,1)}, bf16[128,4096]{1,0:T(8,128)(2,1)}, bf16[512,1024]{1,0:T(8,128)(2,1)}) async-done(((bf16[128,3072]{1,0:T(8,128)(2,1)}, bf16[128,1024]{1,0:T(8,128)(2,1)}, bf16[128,4096]{1,0:T(8,128)(2,1)}, bf16[512,1024]{1,0:T(8,128)(2,1)}), (bf16[128,3072]{1,0:T(8,128)(2,1)}, bf16[128,1024]{1,0:T(8,128)(2,1)}, ...) | async-done | bytes 3145744 | tf_op jit(solution)/shard_map/psum | solution.py:350
  (187 shorter events, 66.4 us)
Async XLA Ops:
  7.2 16.1 %copy-start = (bf16[128,6144]{1,0:T(8,128)(2,1)S(1)}, bf16[128,6144]{1,0:T(8,128)(2,1)}, u32[]{:S(2)}) copy-start(bf16[128,6144]{1,0:T(8,128)(2,1)} %param.15) | copy-start | bytes 4718596
  7.2 71.8 %all-reduce.6.cloned.1.call-start = ((), (), s32[]{:S(2)}) async-start(), calls=%async_computation.17 | async-start | bytes 393216
  24.8 100.8 %all-gather.10.cloned.1.call-start = ((), (), s32[]{:S(2)}) async-start(), calls=%async_computation.9 | async-start | bytes 7077888 | tf_op jit(solution)/shard_map/all_gather | solution.py:255
  25.6 162.4 %all-gather.12.cloned.1.call-start = ((), (), s32[]{:S(2)}) async-start(), calls=%async_computation.10 | async-start | bytes 2359296 | tf_op jit(solution)/shard_map/all_gather | solution.py:256
  26.3 185.1 %all-gather.14.cloned.1.call-start = ((), (), s32[]{:S(2)}) async-start(), calls=%async_computation.11 | async-start | bytes 9437184 | tf_op jit(solution)/shard_map/all_gather | solution.py:257
  26.9 240.5 %all-gather.16.cloned.1.call-start = ((), (), s32[]{:S(2)}) async-start(), calls=%async_computation.12 | async-start | bytes 9437184 | tf_op jit(solution)/shard_map/all_gather | solution.py:258
  28.3 2.3 collective-permute-start
  29.8 105.1 %collective-permute-start.3 = (bf16[2,128,1024]{2,1,0:T(8,128)(2,1)S(1)}, bf16[2,128,1024]{2,1,0:T(8,128)(2,1)}, u32[]{:S(2)}, u32[]{:S(2)}) collective-permute-start(bf16[2,128,1024]{2,1,0:T(8,128)(2,1)S(1)} %dynamic-slice_bitcast_fusion.1), channel_id=1, source_target_pairs={{0,4},{4,0},{8,12},{12,8},{16,20},{20,16},{24,28},{28,24},{1,5},{5... | collective-permute-start | bytes 1572872 | tf_op jit(solution)/shard_map/ppermute | solution.py:200
  31.7 6.0 copy-start.25
  32.8 47.8 %all-to-all-start = ((bf16[4,128,1024]{2,1,0:T(8,128)(2,1)}), bf16[4,128,1024]{2,1,0:T(8,128)(2,1)S(1)}, u32[]{:S(2)}, u32[]{:S(2)}) async-start(bf16[4,128,1024]{2,1,0:T(8,128)(2,1)} %pad_maximum_fusion.2), calls=%async_computation | async-start | bytes 2097152 | tf_op jit(solution)/shard_map/all_to_all | solution.py:218
  134.6 34.5 %collective-permute-start.1 = (bf16[512,2048]{1,0:T(8,128)(2,1)}, bf16[512,2048]{1,0:T(8,128)(2,1)}, u32[]{:S(2)}, u32[]{:S(2)}) collective-permute-start(bf16[512,2048]{1,0:T(8,128)(2,1)} %slice.122), channel_id=1, source_target_pairs={{0,4},{4,0},{8,12},{12,8},{16,20},{20,16},{24,28},{28,24},{1,5},{5... | collective-permute-start | bytes 6291464 | tf_op jit(solution)/shard_map/ppermute | solution.py:200
  137.0 30.7 %all-to-all-start.2 = ((bf16[4,128,1024]{2,1,0:T(8,128)(2,1)}), bf16[4,128,1024]{2,1,0:T(8,128)(2,1)S(1)}, u32[]{:S(2)}, u32[]{:S(2)}) async-start(bf16[4,128,1024]{2,1,0:T(8,128)(2,1)} %pad_maximum_fusion.4), calls=%async_computation.2 | async-start | bytes 2097152 | tf_op jit(solution)/shard_map/all_to_all | solution.py:218
  141.6 319.7 %reduce-scatter.7.cloned.1.call-start = ((), (), s32[]{:S(2)}) async-start(), calls=%async_computation.14 | async-start | bytes 2359296 | tf_op jit(solution)/shard_map/reduce_scatter | solution.py:349
  211.4 56.0 %copy-start.18 = (bf16[512,1024]{1,0:T(8,128)(2,1)S(1)}, bf16[512,1024]{1,0:T(8,128)(2,1)}, u32[]{:S(2)}) copy-start(bf16[512,1024]{1,0:T(8,128)(2,1)} %fusion.7) | copy-start | bytes 3145732
  267.4 15.6 %copy-start.14 = (f32[512,1024]{1,0:T(8,128)S(1)}, f32[512,1024]{1,0:T(8,128)}, u32[]{:S(2)}) copy-start(f32[512,1024]{1,0:T(8,128)} %copy-done.13) | copy-start | bytes 6291460
  283.0 9.1 %copy-start.9 = (bf16[4,128,1024]{2,1,0:T(8,128)(2,1)S(1)}, bf16[4,128,1024]{2,1,0:T(8,128)(2,1)}, u32[]{:S(2)}) copy-start(bf16[4,128,1024]{2,1,0:T(8,128)(2,1)} %copy-done.8) | copy-start | bytes 3145732
  283.1 9.1 %copy-start.23 = (bf16[4096,1024]{1,0:T(8,128)(2,1)S(1)}, bf16[4096,1024]{1,0:T(8,128)(2,1)}, u32[]{:S(2)}) copy-start(bf16[4096,1024]{1,0:T(8,128)(2,1)} %all-gather.16.cloned.1.call-done) | copy-start | bytes 25165828
  283.1 9.2 %copy-start.26 = (f32[512,1024]{1,0:T(8,128)S(1)}, f32[512,1024]{1,0:T(8,128)}, u32[]{:S(2)}) copy-start(f32[512,1024]{1,0:T(8,128)} %get-tuple-element.75) | copy-start | bytes 6291460
  292.2 10.1 %copy-start.24 = (bf16[1024,1024]{1,0:T(8,128)(2,1)S(1)}, bf16[1024,1024]{1,0:T(8,128)(2,1)}, u32[]{:S(2)}) copy-start(bf16[1024,1024]{1,0:T(8,128)(2,1)} %all-gather.12.cloned.1.call-done) | copy-start | bytes 6291460
  302.3 40.5 %copy-start.11 = (f32[512,1024]{1,0:T(8,128)}, f32[512,1024]{1,0:T(8,128)S(1)}, u32[]{:S(2)}) copy-start(f32[512,1024]{1,0:T(8,128)S(1)} %get-tuple-element.52) | copy-start | bytes 6291460
  342.6 4.5 collective-permute-start.4
  345.5 115.9 %reduce-scatter.5.cloned.1.call-start = ((), (), s32[]{:S(2)}) async-start(), calls=%async_computation.13 | async-start | bytes 7077888 | tf_op jit(solution)/shard_map/reduce_scatter | solution.py:349
  357.1 169.9 %reduce-scatter.9.cloned.1.call-start = ((), (), s32[]{:S(2)}) async-start(), calls=%async_computation.15 | async-start | bytes 9437184 | tf_op jit(solution)/shard_map/reduce_scatter | solution.py:349
  368.0 233.9 %reduce-scatter.11.cloned.1.call-start = ((), (), s32[]{:S(2)}) async-start(), calls=%async_computation.16 | async-start | bytes 9437184 | tf_op jit(solution)/shard_map/reduce_scatter | solution.py:349
  381.7 30.9 %all-to-all-start.1 = ((bf16[4,128,1024]{2,1,0:T(8,128)(2,1)}), bf16[4,128,1024]{2,1,0:T(8,128)(2,1)}, u32[]{:S(2)}, u32[]{:S(2)}) async-start(bf16[4,128,1024]{2,1,0:T(8,128)(2,1)} %bitcast.154), calls=%async_computation.1 | async-start | bytes 2097152 | tf_op jit(solution)/shard_map/all_to_all | solution.py:222
  414.5 7.8 %copy-start.7 = (bf16[4,128,1024]{2,1,0:T(8,128)(2,1)S(1)}, bf16[4,128,1024]{2,1,0:T(8,128)(2,1)}, u32[]{:S(2)}) copy-start(bf16[4,128,1024]{2,1,0:T(8,128)(2,1)} %copy-done.6) | copy-start | bytes 3145732
  414.5 7.8 %copy-start.12 = (f32[512,1024]{1,0:T(8,128)S(1)}, f32[512,1024]{1,0:T(8,128)}, u32[]{:S(2)}) copy-start(f32[512,1024]{1,0:T(8,128)} %copy-done.11) | copy-start | bytes 6291460
  414.5 250.0 %collective-permute-start.2 = (bf16[2,128,1024]{2,1,0:T(8,128)(2,1)}, bf16[2,128,1024]{2,1,0:T(8,128)(2,1)}, u32[]{:S(2)}, u32[]{:S(2)}) collective-permute-start(bf16[2,128,1024]{2,1,0:T(8,128)(2,1)} %dynamic-slice_bitcast_fusion.2), channel_id=1, source_target_pairs={{0,4},{4,0},{8,12},{12,8},{16,20},{20,16},{24,28},{28,24},{1,5},{5... | collective-permute-start | bytes 1572872 | tf_op jit(solution)/shard_map/ppermute | solution.py:200
  424.0 235.5 %all-to-all-start.3 = ((bf16[4,128,1024]{2,1,0:T(8,128)(2,1)}), bf16[4,128,1024]{2,1,0:T(8,128)(2,1)}, u32[]{:S(2)}, u32[]{:S(2)}) async-start(bf16[4,128,1024]{2,1,0:T(8,128)(2,1)} %bitcast.152), calls=%async_computation.3 | async-start | bytes 2097152 | tf_op jit(solution)/shard_map/all_to_all | solution.py:222
  428.3 297.5 %all-reduce.8.cloned.1.call-start = ((), (), s32[]{:S(2)}) async-start(), calls=%async_computation.18 | async-start | bytes 6291456 | tf_op jit(solution)/shard_map/psum | solution.py:350
  659.6 8.0 %all-to-all-start.4 = ((f32[8,2,128]{2,1,0:T(2,128)}), f32[8,2,128]{2,1,0:T(2,128)S(1)}, u32[]{:S(2)}, u32[]{:S(2)}) async-start(f32[8,2,128]{2,1,0:T(2,128)} %copy.34), calls=%async_computation.4 | async-start | bytes 16384 | tf_op jit(solution)/shard_map/all_to_all | solution.py:341
  664.0 4.2 collective-permute-start.5
  (16 other events, 40.0 us)
Sparse Core Ops, SparseCore 0:
  24.9 53.9 all-reduce.5
  80.9 44.7 all-gather.9
  127.6 27.7 all-gather.11
  157.1 54.2 all-gather.13
  213.1 54.2 all-gather.15
  345.6 41.0 reduce-scatter.6
  390.1 61.7 reduce-scatter.4
  455.4 71.4 reduce-scatter.8
  530.4 71.4 reduce-scatter.10
  604.4 121.3 all-reduce.7

commit v2 on v1

--- a/solution.py
+++ b/solution.py
@@ -150,6 +150,335 @@
     )(projected, projected, *others, projected, *others, grad, attended, logsum)
 
 
+MESH_ID = pl.DeviceIdType.MESH
+CHUNKS = 12
+
+
+class Gather:
+    SLOTS = 9
+
+    def __init__(self, local, whole, send, recv):
+        self.local, self.whole, self.send, self.recv = local, whole, send, recv
+        self.d = lax.axis_index("dp")
+        self.z = lax.axis_index("seq")
+        self.depth = local.shape[1]
+        self.pending = []
+
+    def _peer(self, flip):
+        return (jnp.bitwise_xor(self.d, flip), self.z)
+
+    def _copy(self, chunk, slot, flip, block_flip, lo, size, own=False):
+        row = jnp.bitwise_xor(self.d, block_flip) * self.depth + lo
+        row = pl.multiple_of(row, 64)
+        dst = self.whole.at[chunk, pl.ds(row, size), :]
+        src = self.local.at[chunk] if own else dst
+        return pltpu.make_async_remote_copy(
+            src_ref=src,
+            dst_ref=dst,
+            send_sem=self.send.at[chunk, slot],
+            recv_sem=self.recv.at[chunk, slot],
+            device_id=self._peer(flip),
+            device_id_type=MESH_ID,
+        )
+
+    def _start(self, *args, **kw):
+        copy = self._copy(*args, **kw)
+        copy.start()
+        self.pending.append(copy)
+
+    def _arrived(self, chunk, slot, block_flip, lo, size):
+        self._copy(chunk, slot, 1, block_flip, lo, size).wait_recv()
+
+    def begin(self, i):
+        n = self.depth
+        self._start(i, 0, 2, 0, 0, n, own=True)
+        self._start(i, 1, 4, 0, 0, n, own=True)
+        self._start(i, 2, 1, 0, 0, n, own=True)
+
+    def relay(self, i):
+        n, h = self.depth, self.depth // 2
+        self._arrived(i, 0, 2, 0, n)
+        self._start(i, 5, 4, 2, 0, h)
+        self._arrived(i, 1, 4, 0, n)
+        self._start(i, 6, 2, 4, h, h)
+        self._start(i, 3, 1, 2, 0, n)
+        self._start(i, 4, 1, 4, 0, n)
+
+    def share(self, i):
+        h = self.depth // 2
+        self._arrived(i, 5, 6, 0, h)
+        self._start(i, 7, 1, 6, 0, h)
+        self._arrived(i, 6, 6, h, h)
+        self._start(i, 8, 1, 6, h, h)
+
+    def finish(self, i):
+        n, h = self.depth, self.depth // 2
+        self._arrived(i, 2, 1, 0, n)
+        self._arrived(i, 3, 3, 0, n)
+        self._arrived(i, 4, 5, 0, n)
+        self._arrived(i, 7, 7, 0, h)
+        self._arrived(i, 8, 7, h, h)
+
+    def drain(self):
+        for copy in self.pending:
+            copy.wait_send()
+        self.pending = []
+
+
+def greet(peers):
+    barrier = pltpu.get_barrier_semaphore()
+    for peer in peers:
+        pl.semaphore_signal(barrier, inc=1, device_id=peer, device_id_type=MESH_ID)
+    pl.semaphore_wait(barrier, len(peers))
+
+
+def gather_kernel(local, whole, send, recv, place):
+    d, z = lax.axis_index("dp"), lax.axis_index("seq")
+    greet([(jnp.bitwise_xor(d, f), z) for f in (1, 2, 4)])
+    gather = Gather(local, whole, send, recv)
+    puts = []
+    for i in range(CHUNKS):
+        row = pl.multiple_of(d * gather.depth, 128)
+        put = pltpu.make_async_copy(
+            local.at[i], whole.at[i, pl.ds(row, gather.depth), :], place.at[i]
+        )
+        put.start()
+        puts.append(put)
+    for t in range(CHUNKS + 4):
+        if t < CHUNKS:
+            gather.begin(t)
+        if 0 <= t - 1 < CHUNKS:
+            gather.relay(t - 1)
+        if 0 <= t - 3 < CHUNKS:
+            gather.share(t - 3)
+        if 0 <= t - 4 < CHUNKS:
+            gather.finish(t - 4)
+    for put in puts:
+        put.wait()
+    gather.drain()
+
+
+def gather_all(local):
+    depth, cols = local.shape[1:]
+    return pl.pallas_call(
+        gather_kernel,
+        out_shape=jax.ShapeDtypeStruct((CHUNKS, 8 * depth, cols), HALF),
+        in_specs=[pl.BlockSpec(memory_space=pltpu.VMEM)],
+        out_specs=pl.BlockSpec(memory_space=pl.ANY),
+        scratch_shapes=[
+            pltpu.SemaphoreType.DMA((CHUNKS, Gather.SLOTS)),
+            pltpu.SemaphoreType.DMA((CHUNKS, Gather.SLOTS)),
+            pltpu.SemaphoreType.DMA((CHUNKS,)),
+        ],
+        compiler_params=pltpu.CompilerParams(
+            collective_id=1, has_side_effects=True, vmem_limit_bytes=32 << 20
+        ),
+        name="gather_all",
+    )(local)
+
+
+class Reduce:
+    SLOTS = 8
+
+    def __init__(self, bufs, sems):
+        (self.own, self.rc, self.s, self.rx, self.ry, self.t, self.ry2, self.rx2, self.r, self.rz1, self.q, self.rz2, self.out) = bufs
+        self.send, self.recv, self.load = sems
+        self.d = lax.axis_index("dp")
+        self.z = lax.axis_index("seq")
+        self.c = self.d % 2
+        self.x = self.d // 2 % 2
+        self.y = self.d // 4
+        self.h = self.z % 2
+        self.depth = self.out.shape[1]
+        self.cols = self.out.shape[2]
+        self.pending = {}
+
+    def _remote(self, i, slot, src, dst, peer):
+        copy = pltpu.make_async_remote_copy(
+            src_ref=src,
+            dst_ref=dst,
+            send_sem=self.send.at[i, slot],
+            recv_sem=self.recv.at[i, slot],
+            device_id=peer,
+            device_id_type=MESH_ID,
+        )
+        copy.start()
+        self.pending[(i, slot)] = copy
+
+    def _plane(self, flip):
+        return (jnp.bitwise_xor(self.d, flip), self.z)
+
+    def _line(self, flip):
+        return (self.d, jnp.bitwise_xor(self.z, flip))
+
+    def sent(self, i, slot):
+        self.pending.pop((i, slot)).wait_send()
+
+    def arrived(self, i, slot):
+        self.pending[(i, slot)].wait_recv()
+
+    def begin(self, i, grads):
+        self._remote(i, 0, grads.at[:, 1 - self.c], self.rc.at[i], self._plane(1))
+        self.fetch = getattr(self, "fetch", {})
+        copy = pltpu.make_async_copy(grads.at[:, self.c], self.own.at[i % 3], self.load.at[i % 3])
+        copy.start()
+        self.fetch[i] = copy
+
+    def plane(self, i):
+        slot, half = i % 3, self.cols // 2
+        self.fetch.pop(i).wait()
+        self.arrived(i, 0)
+        if i >= 3:
+            self.sent(i - 3, 1)
+            self.sent(i - 3, 2)
+
+        @pl.loop(0, 4)
+        def _(k):
+            self.s[slot, k] = (
+                self.own[slot, k].astype(F32) + self.rc[i, k].astype(F32)
+            ).astype(HALF)
+
+        self._remote(
+            i, 1, self.s.at[slot].reshape(2, 2, self.depth, self.cols).at[:, 1 - self.x, :, pl.ds(0, half)],
+            self.rx.at[i], self._plane(2),
+        )
+        self._remote(
+            i, 2, self.s.at[slot].reshape(2, 2, self.depth, self.cols).at[1 - self.y, :, :, pl.ds(half, half)],
+            self.ry.at[i], self._plane(4),
+        )
+
+    def cross(self, i):
+        slot, half = i % 3, self.cols // 2
+        self.arrived(i, 1)
+        self.arrived(i, 2)
+        if i >= 3:
+            self.sent(i - 3, 3)
+            self.sent(i - 3, 4)
+        for k in range(2):
+            self.t[slot, 0, k] = (
+                self.s[slot, 2 * k + self.x, :, pl.ds(0, half)].astype(F32)
+                + self.rx[i, k].astype(F32)
+            ).astype(HALF)
+            self.t[slot, 1, k] = (
+                self.s[slot, 2 * self.y + k, :, pl.ds(half, half)].astype(F32)
+                + self.ry[i, k].astype(F32)
+            ).astype(HALF)
+        self._remote(i, 3, self.t.at[slot, 0, 1 - self.y], self.ry2.at[i], self._plane(4))
+        self._remote(i, 4, self.t.at[slot, 1, 1 - self.x], self.rx2.at[i], self._plane(2))
+
+    def line(self, i):
+        slot, half = i % 3, self.cols // 2
+        rows = self.depth // 2
+        self.arrived(i, 3)
+        self.arrived(i, 4)
+        if i >= 3:
+            self.sent(i - 3, 5)
+        self.r[slot, :, pl.ds(0, half)] = (
+            self.t[slot, 0, self.y].astype(F32) + self.ry2[i].astype(F32)
+        ).astype(HALF)
+        self.r[slot, :, pl.ds(half, half)] = (
+            self.t[slot, 1, self.x].astype(F32) + self.rx2[i].astype(F32)
+        ).astype(HALF)
+        away = pl.multiple_of((1 - self.h) * rows, rows)
+        self._remote(i, 5, self.r.at[slot, pl.ds(away, rows), :], self.rz1.at[i], self._line(1))
+
+    def far(self, i):
+        slot, rows = i % 3, self.depth // 2
+        self.arrived(i, 5)
+        if i >= 3:
+            self.sent(i - 3, 6)
+        mine = pl.multiple_of(self.h * rows, rows)
+        self.q[slot] = (
+            self.r[slot, pl.ds(mine, rows), :].astype(F32) + self.rz1[i].astype(F32)
+        ).astype(HALF)
+        self._remote(i, 6, self.q.at[slot], self.rz2.at[i], self._line(2))
+
+    def close(self, i):
+        slot, rows = i % 3, self.depth // 2
+        self.arrived(i, 6)
+        mine = pl.multiple_of(self.h * rows, rows)
+        self.out[i, pl.ds(mine, rows), :] = (
+            self.q[slot].astype(F32) + self.rz2[i].astype(F32)
+        ).astype(HALF)
+        here = self.out.at[i, pl.ds(mine, rows), :]
+        self._remote(i, 7, here, here, self._line(1))
+
+    def finish(self, i):
+        self.arrived(i, 7)
+
+    def drain(self):
+        for copy in self.pending.values():
+            copy.wait_send()
+        self.pending = {}
+
+
+REDUCE_LAG = (0, 1, 2, 4, 6, 8, 10)
+
+
+def reduce_steps(red, grads_of, t):
+    steps = (
+        lambda i: red.begin(i, grads_of(i)),
+        red.plane,
+        red.cross,
+        red.line,
+        red.far,
+        red.close,
+        red.finish,
+    )
+    for lag, step in zip(REDUCE_LAG, steps):
+        if 0 <= t - lag < CHUNKS:
+            step(t - lag)
+
+
+def reduce_kernel(grads, out, *scratch):
+    d, z = lax.axis_index("dp"), lax.axis_index("seq")
+    greet(
+        [(jnp.bitwise_xor(d, f), z) for f in (1, 2, 4)]
+        + [(d, jnp.bitwise_xor(z, f)) for f in (1, 2)]
+    )
+    red = Reduce(scratch[:12] + (out,), scratch[12:])
+    for t in range(CHUNKS + REDUCE_LAG[-1]):
+        reduce_steps(red, lambda i: grads.at[i], t)
+    red.drain()
+
+
+def reduce_scratch(depth, cols):
+    half, rows = cols // 2, depth // 2
+    ring = 3
+    return [
+        pltpu.VMEM((ring, 4, depth, cols), HALF),
+        pltpu.VMEM((CHUNKS, 4, depth, cols), HALF),
+        pltpu.VMEM((ring, 4, depth, cols), HALF),
+        pltpu.VMEM((CHUNKS, 2, depth, half), HALF),
+        pltpu.VMEM((CHUNKS, 2, depth, half), HALF),
+        pltpu.VMEM((ring, 2, 2, depth, half), HALF),
+        pltpu.VMEM((CHUNKS, depth, half), HALF),
+        pltpu.VMEM((CHUNKS, depth, half), HALF),
+        pltpu.VMEM((ring, depth, cols), HALF),
+        pltpu.VMEM((CHUNKS, rows, cols), HALF),
+        pltpu.VMEM((ring, rows, cols), HALF),
+        pltpu.VMEM((CHUNKS, rows, cols), HALF),
+        pltpu.SemaphoreType.DMA((CHUNKS, Reduce.SLOTS)),
+        pltpu.SemaphoreType.DMA((CHUNKS, Reduce.SLOTS)),
+        pltpu.SemaphoreType.DMA((ring,)),
+    ]
+
+
+def reduce_all(grads):
+    depth, cols = grads.shape[-2:]
+    return pl.pallas_call(
+        reduce_kernel,
+        out_shape=jax.ShapeDtypeStruct((CHUNKS, depth, cols), HALF),
+        in_specs=[pl.BlockSpec(memory_space=pl.ANY)],
+        out_specs=pl.BlockSpec(memory_space=pltpu.VMEM),
+        scratch_shapes=reduce_scratch(depth, cols),
+        compiler_params=pltpu.CompilerParams(
+            collective_id=2, has_side_effects=True, vmem_limit_bytes=58 << 20
+        ),
+        name="reduce_all",
+    )(grads)
+
+
 def norm_parts(rows):
     centred = rows - jnp.mean(rows, axis=-1, keepdims=True)
     variance = jnp.mean(centred * centred, axis=-1, keepdims=True)
@@ -252,10 +581,30 @@
     modulation = (modulation + ada_bias_full).reshape(6, 1, width)
     shift_a, scale_a, gate_a, shift_b, scale_b, gate_b = [modulation[i] for i in range(6)]
 
-    qkv_full = lax.all_gather(qkv_weight, "dp", axis=0, tiled=True)
-    out_full = lax.all_gather(out_weight, "dp", axis=0, tiled=True)
-    up_full = lax.all_gather(up_weight, "dp", axis=0, tiled=True)
-    down_full = lax.all_gather(down_weight, "dp", axis=0, tiled=True)
+    own = dp == 8 and seq == 4 and lats == 2
+    wide = up_bias.shape[0] * dp
+    if own:
+        cut = wide // (4 * dp)
+        local = jnp.concatenate(
+            [
+                qkv_weight.reshape(depth, 3, width).transpose(1, 0, 2),
+                out_weight[None],
+                up_weight.reshape(depth, dp, 4, cut).transpose(2, 0, 1, 3).reshape(4, depth, width),
+                down_weight.reshape(4, cut, width),
+            ],
+            axis=0,
+        )
+        whole = gather_all(local)
+        qkv_full = whole[:3].transpose(1, 0, 2).reshape(width, 3 * width)
+        out_full = whole[3]
+        up_full = whole[4:8].transpose(1, 0, 2).reshape(width, wide)
+        down_full = whole[8:].reshape(wide, width)
+        up_bias_full = up_bias_full.reshape(dp, 4, cut).transpose(1, 0, 2).reshape(-1)
+    else:
+        qkv_full = lax.all_gather(qkv_weight, "dp", axis=0, tiled=True)
+        out_full = lax.all_gather(out_weight, "dp", axis=0, tiled=True)
+        up_full = lax.all_gather(up_weight, "dp", axis=0, tiled=True)
+        down_full = lax.all_gather(down_weight, "dp", axis=0, tiled=True)
 
     rows = spread(tokens).astype(F32)
     cot = spread(cotangent).astype(F32)
@@ -349,6 +698,27 @@
         share = lax.psum_scatter(grad, "dp", scatter_dimension=0, tiled=True)
         return lax.psum(share, "seq").astype(F32)
 
+    if own:
+        up_bias_grad = up_bias_grad.reshape(4, dp, cut).transpose(1, 0, 2).reshape(-1)
+        grads = jnp.concatenate(
+            [
+                qkv_weight_grad.reshape(width, 3, width).transpose(1, 0, 2),
+                out_weight_grad[None],
+                up_weight_grad.reshape(width, 4, width).transpose(1, 0, 2),
+                down_weight_grad.reshape(4, width, width),
+            ],
+            axis=0,
+        )
+        shares = reduce_all(grads.reshape(CHUNKS, dp // 2, 2, depth, width)).astype(F32)
+        qkv_g = shares[:3].transpose(1, 0, 2).reshape(depth, 3 * width)
+        out_g = shares[3]
+        up_g = shares[4:8].reshape(4, depth, dp, cut).transpose(1, 2, 0, 3).reshape(depth, wide)
+        down_g = shares[8:].reshape(4 * cut, width)
+    else:
+        qkv_g, out_g, up_g, down_g = map(
+            reduce_weight, (qkv_weight_grad, out_weight_grad, up_weight_grad, down_weight_grad)
+        )
+
     bias_parts = jnp.concatenate(
         [
             b.reshape(dp, -1)
@@ -366,13 +736,13 @@
         condition_grad,
         ada_weight_grad,
         ada_bias_grad,
-        reduce_weight(qkv_weight_grad),
+        qkv_g,
         qv_g,
-        reduce_weight(out_weight_grad),
+        out_g,
         ob_g,
-        reduce_weight(up_weight_grad),
+        up_g,
         ub_g,
-        reduce_weight(down_weight_grad),
+        down_g,
         db_g,
     )
 

time: 747 us -> 736 us (0.985)
  waiting for transfers between devices: 396 us -> 24.3 us
  Pallas kernels: 54.8 us -> 314 us
  local copies, waits for them, and re-layouts: 24.8 us -> 127 us
  other arithmetic: 29.1 us -> 55.5 us
  blocking collectives: 91.7 us -> 70.1 us
    pallas_call x0 -> x2, Pallas kernels: none -> 260 us  [the longest x1 151 us: reduce_all(): pl.pallas_call(reduce_kernel, out_shape=jax.ShapeDtypeStruct((CHUNKS, dep...]
    reduce_scatter x4 -> x0, waiting for transfers between devices: 141 us -> none  [reduce_weight(): share = lax.psum_scatter(grad, 'dp', scatter_dimension=0, tiled=True)]
    all_gather x4 -> x0, waiting for transfers between devices: 104 us -> none  [the longest x1 43.9 us: body(): down_full = lax.all_gather(down_weight, 'dp', axis=0, tiled=True)]
    psum x1 -> x0, waiting for transfers between devices: 54.8 us -> none  [reduce_weight(): return lax.psum(share, 'seq').astype(F32)]
    transpose x0 -> x9, local copies, waits for them, and re-layouts: none -> 53.8 us  [the longest x2 22.9 us: body(): up_full = whole[4:8].transpose(1, 0, 2).reshape(width, wide)]
    unnamed x11 -> x2, waiting for transfers between devices: 43.2 us -> 0.04 us
    all_to_all x2, waiting for transfers between devices: 24.8 us -> 0.01 us  [collect(): both = lax.all_to_all(both, 'seq', 0, 0, tiled=True)]
    reshape x1 -> x6, local copies, waits for them, and re-layouts: 0.01 us -> 20.5 us  [the longest x1 7.92 us: body(): up_weight_grad.reshape(width, 4, width).transpose(1, 0, 2)]
  transfers between devices with their start and end apart: 21 -> 12, of which waited for: 12 -> 1; matrix products, arithmetic and copies ran while one was open for 14% -> 27% of each run, Pallas kernels for 3% -> 41%
where the time goes in v2:
time: 736 us; the launch traced here: 727 us
  Pallas kernels  314 us (43%)
  local copies, waits for them, and re-layouts  127 us (17%)
  matrix products  97.2 us (13%)
  blocking collectives  70.1 us (10%)
  other arithmetic  55.5 us (8%)
  starting transfers between devices  24.3 us (3%)
  waiting for transfers between devices  24.3 us (3%)
  between operations  15 us (2%)
    pallas_call x1, Pallas kernels, reduce_all(): pl.pallas_call(reduce_kernel, out_shape=jax.ShapeDtypeStruct((CHUNKS, dep...  151 us
    pallas_call x1, Pallas kernels, gather_all(): pl.pallas_call(gather_kernel, out_shape=jax.ShapeDtypeStruct((CHUNKS, 8 *...  109 us
    dot_general x5, matrix products, nt(): lax.dot_general(a, b, (((1,), (1,)), ((), ())), preferred_element_type=F32)  38.5 us
    pallas_call x1, Pallas kernels, attend_grad(): pl.pallas_call(functools.partial(attend_grad_kernel, groups), grid=(tiles...  36.1 us
    dot_general x5, matrix products, nn(): return jnp.dot(a, b, preferred_element_type=F32)  31.6 us
    dot_general x5, matrix products, tn(): lax.dot_general(a, b, (((0,), (0,)), ((), ())), preferred_element_type=F32)  27.1 us
    all_to_all x2, waiting for transfers between devices, spread(): return lax.all_to_all(both, 'seq', 0, 0, tiled=True).reshape(-1, width)  24.2 us
    unnamed x1, blocking collectives  24 us
  transfers between devices with their start and end apart: 12, of which 1 were waited for; matrix products, arithmetic and copies ran while one was open for 27% of the time, Pallas kernels for 41%

profile of v2, /device:TPU:0, one launch (start us, length us, event | category | flops | bytes accessed | tf_op | source)
XLA Modules:
  0.0 727.4 jit_solution(14998920026660750423)
XLA Ops:
  14.9 10.3 %all-gather.3 = bf16[8,1,3840]{2,1,0:T(2,128)(2,1)S(1)} all-gather(bf16[1,1,3840]{2,1,0:T(2,128)(2,1)S(1)} %reshape.328), channel_id=2, replica_groups=mesh['dp'=8,'seq'=4] {'dp'}, dimensions={0}, use_global_device_ids=true | all-gather | bytes 69120 | tf_op jit(solution)/shard_map/all_gather | solution.py:563
  32.4 4.9 all-to-all-start
  51.7 108.6 %gather_all.1 = bf16[12,1024,1024]{2,1,0:T(8,128)(2,1)} custom-call(bf16[12,128,1024]{2,1,0:T(8,128)(2,1)S(1)} %pad_maximum_fusion.1.local), custom_call_target="tpu_custom_call" | custom-call | tf_op jit(solution)/shard_map/gather_all/pallas_call | solution.py:263
  160.4 6.2 slice_bitcast_fusion.1
  166.6 8.6 %copy.49 = bf16[1024,3,1024]{0,2,1:T(8,128)(2,1)} copy(bf16[1024,3,1024]{2,0,1:T(8,128)(2,1)} %slice_bitcast_fusion.1) | data formatting | bytes 12582912 | tf_op jit(solution)/shard_map/transpose | solution.py:598
  178.2 5.3 all-to-all-start.2
  185.8 24.2 %all-to-all-done.2 = bf16[4,128,1024]{2,1,0:T(8,128)(2,1)} async-done(((bf16[4,128,1024]{2,1,0:T(8,128)(2,1)}), bf16[4,128,1024]{2,1,0:T(8,128)(2,1)}, u32[]{:S(2)}, u32[]{:S(2)}) %all-to-all-start.2) | async-done | bytes 1048608 | tf_op jit(solution)/shard_map/all_to_all | solution.py:547
  213.5 6.5 add_convert_fusion.refs_0_.refs_1_.refs_3_
  223.2 11.6 %slice_bitcast_fusion = (bf16[1024,4,1024]{2,0,1:T(8,128)(2,1)}, bf16[4,1024,1024]{2,1,0:T(8,128)(2,1)}) fusion(bf16[12,1024,1024]{2,1,0:T(8,128)(2,1)} %gather_all.1), kind=kLoop, calls=%fused_computation.11 | loop fusion | bytes 33554432 | tf_op jit(solution)/shard_map/transpose | solution.py:600
  234.8 11.3 %copy.50 = bf16[1024,4,1024]{0,2,1:T(8,128)(2,1)} copy(bf16[1024,4,1024]{2,0,1:T(8,128)(2,1)} %get-tuple-element.70) | data formatting | bytes 16777216 | tf_op jit(solution)/shard_map/transpose | solution.py:600
  247.5 18.4 %attend.1 = (bf16[512,1024]{1,0:T(8,128)(2,1)S(1)}, f32[128,512]{1,0:T(8,128)S(1)}) custom-call(bf16[512,3072]{1,0:T(8,128)(2,1)} %copy-done.4, bf16[512,3072]{1,0:T(8,128)(2,1)} %copy-done.4, bf16[512,2048]{1,0:T(8,128)(2,1)} %collective-permute-done.1.refs_2_.refs_4_, bf16[512,3072]{1,0:T(8,128)(2,1)} %copy-done.4, ...), custom_call_target="tpu_custom_call" | custom-call | tf_op jit(solution)/shard_map/attend/pallas_call | solution.py:69
  269.8 7.1 fusion.65
  276.9 15.9 %fusion.67 = (f32[4096]{0:T(1024)S(1)}, bf16[512,4096]{1,0:T(8,128)(2,1)}) fusion(f32[512,4096]{1,0:T(8,128)} %fusion.65, f32[4096]{0:T(1024)S(1)} %convert_bitcast_fusion, bf16[512,1024]{1,0:T(8,128)(2,1)S(1)} %bitcast.237, bf16[4096,1024]{1,0:T(8,128)(2,1)} %bitcast.226), kind=kOutput, calls=%fused_computation.162 | convolution fusion | flops 4341100544 | bytes 22052864 | tf_op jit(solution)/shard_map/dot_general | solution.py:22
  292.8 8.4 %multiply_reduce_fusion = (f32[1024]{0:T(1024)S(1)}, f32[512]{0:T(512)S(1)}, f32[512]{0:T(512)S(1)}, f32[1024]{0:T(1024)S(1)}, f32[512,1024]{1,0:T(8,128)}) fusion(f32[512,1024]{1,0:T(8,128)S(1)} %get-tuple-element.69, f32[512]{0:T(512)S(1)} %add_rsqrt_fusion, f32[512]{0:T(512)S(1)} %broadcast_multiply_fusion.4, f32[1024]{0:T(1024)S(1)} %get-tuple-element.95, ...), kind=kOutput, calls=%fused_computation.59 | convolution fusion | flops 4299682816 | bytes 16797696 | tf_op jit(solution)/shard_map/dot_general | solution.py:22
  301.2 14.3 %fusion.8 = (f32[1024]{0:T(1024)S(1)}, bf16[512,1024]{1,0:T(8,128)(2,1)}, f32[1024]{0:T(1024)S(1)}, f32[1024]{0:T(1024)S(1)}, f32[512,1024]{1,0:T(8,128)S(1)}, /*index=5*/bf16[512,1024]{1,0:T(8,128)(2,1)}) fusion(bf16[4,128,1024]{2,1,0:T(8,128)(2,1)} %all-to-all-done.2, f32[1024]{0:T(1024)S(1)} %get-tuple-element.91, ...), kind=kOutput, calls=%fused_computation.30 | convolution fusion | flops 4327470080 | bytes 28368896 | tf_op jit(solution)/shard_map/dot_general | solution.py:18
  315.5 4.6 fusion.40.refs_5_
  322.7 7.3 %convolution_convert_fusion.1 = bf16[1024,4096]{1,0:T(8,128)(2,1)} fusion(bf16[512,4096]{1,0:T(8,128)(2,1)S(1)} %copy-done.25, f32[512,1024]{1,0:T(8,128)S(1)} %get-tuple-element.69, f32[1024]{0:T(1024)S(1)} %get-tuple-element.94, f32[1024]{0:T(1024)S(1)} %get-tuple-element.95, f32[512]{0:T(512)S(1)} %add_rsqrt_fusion, f32[512]{0:T(512)S(1)} %broadcast_multiply_fusion.4), kind=kOutput, calls=%fused_computation.13 | convolution fusion | flops 4301783040 | bytes 14692352 | tf_op jit(solution)/shard_map/dot_general | solution.py:26
  334.5 7.9 %copy.75 = bf16[128,4,8,1024]{3,2,0,1:T(8,128)(2,1)} copy(bf16[128,4,8,1024]{3,2,1,0:T(8,128)(2,1)} %bitcast.222) | data formatting | bytes 16777216 | tf_op jit(solution)/shard_map/reshape | solution.py:707
  342.4 36.1 %attend_grad.1 = (bf16[512,1024]{1,0:T(8,128)(2,1)S(1)}, bf16[512,1024]{1,0:T(8,128)(2,1)S(1)}, bf16[512,1024]{1,0:T(8,128)(2,1)S(1)}, bf16[512,1024]{1,0:T(8,128)(2,1)S(1)}, bf16[512,1024]{1,0:T(8,128)(2,1)S(1)}) custom-call(bf16[512,3072]{1,0:T(8,128)(2,1)} %copy-done.4, bf16[512,3072]{1,0:T(8,128)(2,1)} %copy-done.4, ...), custom_call_target="tpu_custom_call" | custom-call | tf_op jit(solution)/shard_map/attend_grad/pallas_call | solution.py:138
  382.5 8.6 %convolution_convert_fusion = bf16[4096,1024]{1,0:T(8,128)(2,1)} fusion(bf16[512,1024]{1,0:T(8,128)(2,1)S(1)} %copy-done.27, f32[512,4096]{1,0:T(8,128)S(1)} %bitcast.263, f32[4096]{0:T(1024)S(1)} %convert_bitcast_fusion), kind=kOutput, calls=%fused_computation.12 | convolution fusion | flops 4320133120 | bytes 17842176 | tf_op jit(solution)/shard_map/dot_general | solution.py:26
  396.0 9.1 %fusion.30 = (f32[1024]{0:T(1024)S(1)}, f32[512]{0:T(512)S(1)}, f32[512]{0:T(512)S(1)}, f32[1024]{0:T(1024)S(1)}, bf16[512,1024]{1,0:T(8,128)(2,1)}, /*index=5*/f32[512,1024]{1,0:T(8,128)}) fusion(bf16[4,128,1024]{2,1,0:T(8,128)(2,1)S(1)} %copy-done.7, f32[512]{0:T(512)S(1)} %get-tuple-element.105, f32[512]{0:T(512)S(1)} %get-tuple-element.103, ...), kind=kOutput, calls=%fused_computation.56 | convolution fusion | flops 3234329600 | bytes 13656064 | tf_op jit(solution)/shard_map/dot_general | solution.py:22
  405.2 13.7 %all-gather.1 = f32[24576]{0:T(1024)S(1)} all-gather(f32[6144]{0:T(1024)S(1)} %constant_dynamic-update-slice_fusion), channel_id=3, replica_groups=mesh['dp'=8,'seq'=4] {'seq'}, dimensions={0}, use_global_device_ids=true | all-gather | bytes 122880 | tf_op jit(solution)/shard_map/all_gather | solution.py:679
  419.0 10.1 %all-gather.4 = f32[8,4,6144]{2,1,0:T(4,128)S(1)} all-gather(f32[1,4,6144]{2,1,0:T(4,128)S(1)} %reshape.330), channel_id=4, replica_groups=mesh['dp'=8,'seq'=4] {'dp'}, dimensions={0}, use_global_device_ids=true | all-gather | bytes 884736 | tf_op jit(solution)/shard_map/all_gather | solution.py:680
  430.3 5.3 fusion.43
  435.5 5.6 convolution_convert_fusion.2
  441.1 8.6 %copy.55 = bf16[1024,3072]{0,1:T(8,128)(2,1)} copy(bf16[1024,3072]{1,0:T(8,128)(2,1)} %convolution_convert_fusion.2) | data formatting | bytes 12582912 | tf_op jit(solution)/shard_map/convert_element_type | solution.py:662
  449.7 8.6 %copy.56 = bf16[3,1024,1024]{2,1,0:T(8,128)(2,1)} copy(bf16[3,1024,1024]{1,2,0:T(8,128)(2,1)} %bitcast.217) | data formatting | bytes 12582912 | tf_op jit(solution)/shard_map/transpose | solution.py:705
  458.3 17.5 %pad_maximum_fusion.grads = bf16[12,4,2,128,1024]{4,3,2,1,0:T(8,128)(2,1)} fusion(bf16[4,4,2,128,1024]{4,3,2,1,0:T(8,128)(2,1)} %bitcast.225, bf16[4,4,2,128,1024]{4,3,2,1,0:T(8,128)(2,1)} %bitcast.215, bf16[1,4,2,128,1024]{4,3,2,1,0:T(8,128)(2,1)} %bitcast.234, bf16[3,4,2,128,1024]{4,3,2,1,0:T(8,128)(2,1)} %bitcast.216), kind=kLoop, calls=%fused_computation | loop fusion | flops 37748736 | bytes 50331648 | tf_op jit(solution)/shard_map/concatenate | solution.py:703
  475.8 151.1 %reduce_all.1 = bf16[12,128,1024]{2,1,0:T(8,128)(2,1)} custom-call(bf16[12,4,2,128,1024]{4,3,2,1,0:T(8,128)(2,1)} %pad_maximum_fusion.grads), custom_call_target="tpu_custom_call" | custom-call | tf_op jit(solution)/shard_map/reduce_all/pallas_call | solution.py:469
  637.3 4.5 all-to-all-start.3
  649.0 24.0 %all-reduce.1 = f32[8,1024]{1,0:T(8,128)S(1)} all-reduce(f32[8,1024]{1,0:T(8,128)S(1)} %pad_maximum_fusion.9), channel_id=6, replica_groups=mesh['dp'=8,'seq'=4] {'dp'}, use_global_device_ids=true, to_apply=%region_22.23.clone | all-reduce | flops 8192 | bytes 65536
  673.6 11.9 %psum.7 = f32[1,1024]{1,0:T(1,128)S(1)} all-reduce(f32[1,1024]{1,0:T(1,128)S(1)} %constant_dynamic-slice_fusion.1), channel_id=1, replica_groups=mesh['dp'=8,'seq'=4] {'seq'}, use_global_device_ids=true, to_apply=%region_23.24 | all-reduce | flops 1024 | bytes 8192 | tf_op jit(solution)/shard_map/psum | solution.py:730
  (191 shorter events, 116.0 us)
Async XLA Ops:
  7.2 19.3 %copy-start = (bf16[128,6144]{1,0:T(8,128)(2,1)S(1)}, bf16[128,6144]{1,0:T(8,128)(2,1)}, u32[]{:S(2)}) copy-start(bf16[128,6144]{1,0:T(8,128)(2,1)} %param.15) | copy-start | bytes 4718596
  7.2 176.3 %all-reduce.4.cloned.1.call-start = ((), (), s32[]{:S(2)}) async-start(), calls=%async_computation.5 | async-start | bytes 393216
  9.2 20.9 %copy-start.18 = (bf16[2,256,1024]{2,1,0:T(8,128)(2,1)S(1)}, bf16[2,256,1024]{2,1,0:T(8,128)(2,1)}, u32[]{:S(2)}) copy-start(bf16[2,256,1024]{2,1,0:T(8,128)(2,1)} %param.13) | copy-start | bytes 3145732
  9.2 20.9 %collective-permute-start = (bf16[2,128,1024]{2,1,0:T(8,128)(2,1)}, bf16[2,128,1024]{2,1,0:T(8,128)(2,1)}, u32[]{:S(2)}, u32[]{:S(2)}) collective-permute-start(bf16[2,128,1024]{2,1,0:T(8,128)(2,1)} %dynamic-slice_bitcast_fusion.3), channel_id=1, source_target_pairs={{0,4},{4,0},{8,12},{12,8},{16,20},{20,16},{24,28},{28,24},{1,5},{5... | collective-permute-start | bytes 1572872 | tf_op jit(solution)/shard_map/ppermute | solution.py:529
  29.1 146.7 %collective-permute-start.3 = (bf16[2,128,1024]{2,1,0:T(8,128)(2,1)S(1)}, bf16[2,128,1024]{2,1,0:T(8,128)(2,1)}, u32[]{:S(2)}, u32[]{:S(2)}) collective-permute-start(bf16[2,128,1024]{2,1,0:T(8,128)(2,1)S(1)} %dynamic-slice_bitcast_fusion.1), channel_id=1, source_target_pairs={{0,4},{4,0},{8,12},{12,8},{16,20},{20,16},{24,28},{28,24},{1,5},{5... | collective-permute-start | bytes 1572872 | tf_op jit(solution)/shard_map/ppermute | solution.py:529
  32.4 145.8 %all-to-all-start = ((bf16[4,128,1024]{2,1,0:T(8,128)(2,1)}), bf16[4,128,1024]{2,1,0:T(8,128)(2,1)S(1)}, u32[]{:S(2)}, u32[]{:S(2)}) async-start(bf16[4,128,1024]{2,1,0:T(8,128)(2,1)} %pad_maximum_fusion.4), calls=%async_computation | async-start | bytes 2097152 | tf_op jit(solution)/shard_map/all_to_all | solution.py:547
  42.5 7.2 copy-start.19
  166.6 8.6 %copy-start.24 = (u32[32]{0:T(128)S(1)}, u32[32]{0:T(128)}, u32[]{:S(2)}) copy-start(u32[32]{0:T(128)} %constant.105) | copy-start | bytes 388
  178.2 87.8 %copy-start.6 = (bf16[4,128,1024]{2,1,0:T(8,128)(2,1)}, bf16[4,128,1024]{2,1,0:T(8,128)(2,1)S(1)}, u32[]{:S(2)}) copy-start(bf16[4,128,1024]{2,1,0:T(8,128)(2,1)S(1)} %all-to-all-done) | copy-start | bytes 3145732
  178.2 31.9 %all-to-all-start.2 = ((bf16[4,128,1024]{2,1,0:T(8,128)(2,1)}), bf16[4,128,1024]{2,1,0:T(8,128)(2,1)}, u32[]{:S(2)}, u32[]{:S(2)}) async-start(bf16[4,128,1024]{2,1,0:T(8,128)(2,1)} %pad_maximum_fusion.6), calls=%async_computation.2 | async-start | bytes 2097152 | tf_op jit(solution)/shard_map/all_to_all | solution.py:547
  223.2 24.3 %collective-permute-start.1 = (bf16[512,2048]{1,0:T(8,128)(2,1)}, bf16[512,2048]{1,0:T(8,128)(2,1)}, u32[]{:S(2)}, u32[]{:S(2)}) collective-permute-start(bf16[512,2048]{1,0:T(8,128)(2,1)} %slice.154), channel_id=1, source_target_pairs={{0,4},{4,0},{8,12},{12,8},{16,20},{20,16},{24,28},{28,24},{1,5},{5... | collective-permute-start | bytes 6291464 | tf_op jit(solution)/shard_map/ppermute | solution.py:529
  247.5 22.3 %slice-start = ((s8[8388608]{0:T(1024)(128)(4,1)}), s8[4194304]{0:T(1024)(128)(4,1)S(1)}, s32[]{:S(2)}) async-start(s8[8388608]{0:T(1024)(128)(4,1)} %bitcast.218), calls=%async_computation.6 | async-start | bytes 8388608
  266.0 54.1 %copy-start.3 = (bf16[512,1024]{1,0:T(8,128)(2,1)}, bf16[512,1024]{1,0:T(8,128)(2,1)S(1)}, u32[]{:S(2)}) copy-start(bf16[512,1024]{1,0:T(8,128)(2,1)S(1)} %get-tuple-element.20.refs_6_) | copy-start | bytes 3145732
  269.8 7.1 copy-start.17
  315.5 4.6 copy-start.13
  330.0 61.0 %all-to-all-start.1 = ((bf16[4,128,1024]{2,1,0:T(8,128)(2,1)}), bf16[4,128,1024]{2,1,0:T(8,128)(2,1)}, u32[]{:S(2)}, u32[]{:S(2)}) async-start(bf16[4,128,1024]{2,1,0:T(8,128)(2,1)} %bitcast.22), calls=%async_computation.1 | async-start | bytes 2097152 | tf_op jit(solution)/shard_map/all_to_all | solution.py:551
  342.4 40.1 %slice-start.2 = ((s8[8388608]{0:T(1024)(128)(4,1)}), s8[4194304]{0:T(1024)(128)(4,1)S(1)}, s32[]{:S(2)}) async-start(s8[8388608]{0:T(1024)(128)(4,1)} %bitcast.262), calls=%async_computation.8 | async-start | bytes 8388608
  342.4 40.1 %slice-start.3 = ((s8[8388608]{0:T(1024)(128)(4,1)}), s8[4194304]{0:T(1024)(128)(4,1)S(1)}, s32[]{:S(2)}) async-start(s8[8388608]{0:T(1024)(128)(4,1)} %bitcast.262), calls=%async_computation.9 | async-start | bytes 8388608
  382.0 11.0 %collective-permute-start.4 = (bf16[512,2048]{1,0:T(8,128)(2,1)}, bf16[512,2048]{1,0:T(8,128)(2,1)}, u32[]{:S(2)}, u32[]{:S(2)}) collective-permute-start(bf16[512,2048]{1,0:T(8,128)(2,1)} %pad_maximum_fusion.3), channel_id=1, source_target_pairs={{0,4},{4,0},{8,12},{12,8},{16,20},{20,16},{24,28},{28,24},{1,5},{5... | collective-permute-start | bytes 6291464 | tf_op jit(solution)/shard_map/ppermute | solution.py:529
  392.9 294.5 %collective-permute-start.2 = (bf16[2,128,1024]{2,1,0:T(8,128)(2,1)}, bf16[2,128,1024]{2,1,0:T(8,128)(2,1)}, u32[]{:S(2)}, u32[]{:S(2)}) collective-permute-start(bf16[2,128,1024]{2,1,0:T(8,128)(2,1)} %dynamic-slice_bitcast_fusion.2), channel_id=1, source_target_pairs={{0,4},{4,0},{8,12},{12,8},{16,20},{20,16},{24,28},{28,24},{1,5},{5... | collective-permute-start | bytes 1572872 | tf_op jit(solution)/shard_map/ppermute | solution.py:529
  396.0 9.2 %copy-start.9 = (bf16[512,2048]{1,0:T(8,128)(2,1)}, bf16[512,2048]{1,0:T(8,128)(2,1)S(1)}, u32[]{:S(2)}) copy-start(bf16[512,2048]{1,0:T(8,128)(2,1)S(1)} %add_convert_fusion.1) | copy-start | bytes 6291460
  430.3 5.3 copy-start.10
  430.3 5.3 copy-start.26
  631.2 4.5 copy-start.15
  637.3 58.5 %all-to-all-start.3 = ((bf16[4,128,1024]{2,1,0:T(8,128)(2,1)}), bf16[4,128,1024]{2,1,0:T(8,128)(2,1)}, u32[]{:S(2)}, u32[]{:S(2)}) async-start(bf16[4,128,1024]{2,1,0:T(8,128)(2,1)} %bitcast.36), calls=%async_computation.3 | async-start | bytes 2097152 | tf_op jit(solution)/shard_map/all_to_all | solution.py:551
  644.4 4.5 copy-start.22
  685.5 5.8 copy-start.16
  689.7 4.7 copy-start.11
  695.8 20.8 %all-to-all-start.4 = ((f32[8,2,128]{2,1,0:T(2,128)}), f32[8,2,128]{2,1,0:T(2,128)S(1)}, u32[]{:S(2)}, u32[]{:S(2)}) async-start(f32[8,2,128]{2,1,0:T(2,128)} %copy.54), calls=%async_computation.4 | async-start | bytes 16384 | tf_op jit(solution)/shard_map/all_to_all | solution.py:690
  699.2 6.4 copy-start.12
  701.2 16.0 %collective-permute-start.5 = (bf16[2,128,1024]{2,1,0:T(8,128)(2,1)}, bf16[2,128,1024]{2,1,0:T(8,128)(2,1)}, u32[]{:S(2)}, u32[]{:S(2)}) collective-permute-start(bf16[2,128,1024]{2,1,0:T(8,128)(2,1)} %dynamic-slice_bitcast_fusion), channel_id=1, source_target_pairs={{0,4},{4,0},{8,12},{12,8},{16,20},{20,16},{24,28},{28,24},{1,5},{5... | collective-permute-start | bytes 1572872 | tf_op jit(solution)/shard_map/ppermute | solution.py:529
  711.3 5.3 copy-start.23
  (12 other events, 28.2 us)
Sparse Core Ops, SparseCore 0:
  28.1 54.1 all-reduce.3

commit v3 on v2

--- a/solution.py
+++ b/solution.py
@@ -150,79 +150,67 @@
     )(projected, projected, *others, projected, *others, grad, attended, logsum)
 
 
+def norm_parts(rows):
+    centred = rows - jnp.mean(rows, axis=-1, keepdims=True)
+    variance = jnp.mean(centred * centred, axis=-1, keepdims=True)
+    inverse = lax.rsqrt(variance + EPSILON)
+    return centred * inverse, inverse
+
+
+def norm_grad(grad, hat, inverse, scale):
+    g = grad * (1.0 + scale)
+    return (
+        g
+        - jnp.mean(g, axis=-1, keepdims=True)
+        - hat * jnp.mean(g * hat, axis=-1, keepdims=True)
+    ) * inverse
+
+
+def gelu_tanh(inputs):
+    return jax.nn.gelu(inputs, approximate=True)
+
+
 MESH_ID = pl.DeviceIdType.MESH
 CHUNKS = 12
-
-
-class Gather:
-    SLOTS = 9
-
-    def __init__(self, local, whole, send, recv):
-        self.local, self.whole, self.send, self.recv = local, whole, send, recv
+KEYS, VALUES, QUERIES, OUT, FEED = 0, 1, 2, 3, 4
+
+
+def guarded(low, value, high, run):
+    if isinstance(value, int):
+        if low <= value < high:
+            run(value)
+        return
+
+    @pl.when(jnp.logical_and(value >= low, value < high))
+    def _():
+        run(value)
+
+
+class Place:
+    def __init__(self):
         self.d = lax.axis_index("dp")
         self.z = lax.axis_index("seq")
-        self.depth = local.shape[1]
-        self.pending = []
-
-    def _peer(self, flip):
+        self.c = self.d % 2
+        self.x = self.d // 2 % 2
+        self.y = self.d // 4
+        self.p = self.d // 2
+
+    def plane(self, flip):
         return (jnp.bitwise_xor(self.d, flip), self.z)
 
-    def _copy(self, chunk, slot, flip, block_flip, lo, size, own=False):
-        row = jnp.bitwise_xor(self.d, block_flip) * self.depth + lo
-        row = pl.multiple_of(row, 64)
-        dst = self.whole.at[chunk, pl.ds(row, size), :]
-        src = self.local.at[chunk] if own else dst
-        return pltpu.make_async_remote_copy(
-            src_ref=src,
-            dst_ref=dst,
-            send_sem=self.send.at[chunk, slot],
-            recv_sem=self.recv.at[chunk, slot],
-            device_id=self._peer(flip),
-            device_id_type=MESH_ID,
-        )
-
-    def _start(self, *args, **kw):
-        copy = self._copy(*args, **kw)
-        copy.start()
-        self.pending.append(copy)
-
-    def _arrived(self, chunk, slot, block_flip, lo, size):
-        self._copy(chunk, slot, 1, block_flip, lo, size).wait_recv()
-
-    def begin(self, i):
-        n = self.depth
-        self._start(i, 0, 2, 0, 0, n, own=True)
-        self._start(i, 1, 4, 0, 0, n, own=True)
-        self._start(i, 2, 1, 0, 0, n, own=True)
-
-    def relay(self, i):
-        n, h = self.depth, self.depth // 2
-        self._arrived(i, 0, 2, 0, n)
-        self._start(i, 5, 4, 2, 0, h)
-        self._arrived(i, 1, 4, 0, n)
-        self._start(i, 6, 2, 4, h, h)
-        self._start(i, 3, 1, 2, 0, n)
-        self._start(i, 4, 1, 4, 0, n)
-
-    def share(self, i):
-        h = self.depth // 2
-        self._arrived(i, 5, 6, 0, h)
-        self._start(i, 7, 1, 6, 0, h)
-        self._arrived(i, 6, 6, h, h)
-        self._start(i, 8, 1, 6, h, h)
-
-    def finish(self, i):
-        n, h = self.depth, self.depth // 2
-        self._arrived(i, 2, 1, 0, n)
-        self._arrived(i, 3, 3, 0, n)
-        self._arrived(i, 4, 5, 0, n)
-        self._arrived(i, 7, 7, 0, h)
-        self._arrived(i, 8, 7, h, h)
-
-    def drain(self):
-        for copy in self.pending:
-            copy.wait_send()
-        self.pending = []
+    def line(self, flip):
+        return (self.d, jnp.bitwise_xor(self.z, flip))
+
+
+def remote(src, dst, send, recv, peer):
+    return pltpu.make_async_remote_copy(
+        src_ref=src,
+        dst_ref=dst,
+        send_sem=send,
+        recv_sem=recv,
+        device_id=peer,
+        device_id_type=MESH_ID,
+    )
 
 
 def greet(peers):
@@ -232,49 +220,530 @@
     pl.semaphore_wait(barrier, len(peers))
 
 
-def gather_kernel(local, whole, send, recv, place):
-    d, z = lax.axis_index("dp"), lax.axis_index("seq")
-    greet([(jnp.bitwise_xor(d, f), z) for f in (1, 2, 4)])
-    gather = Gather(local, whole, send, recv)
-    puts = []
-    for i in range(CHUNKS):
-        row = pl.multiple_of(d * gather.depth, 128)
-        put = pltpu.make_async_copy(
-            local.at[i], whole.at[i, pl.ds(row, gather.depth), :], place.at[i]
+class Gather:
+    SENDS = (
+        (2, 0, None),
+        (4, 0, None),
+        (1, 0, None),
+        (1, 2, None),
+        (1, 4, None),
+        (4, 2, 0),
+        (2, 4, 1),
+        (1, 6, 0),
+        (1, 6, 1),
+    )
+
+    def __init__(self, here, whole, send, recv):
+        self.here, self.whole, self.send, self.recv = here, whole, send, recv
+        self.depth = whole.shape[1] // 8
+
+    def _block(self, chunk, flip, half):
+        size = self.depth if half is None else self.depth // 2
+        lo = 0 if half is None else half * size
+        row = pl.multiple_of(jnp.bitwise_xor(self.here.d, flip) * self.depth + lo, 64)
+        return self.whole.at[chunk, pl.ds(row, size), :]
+
+    def _copy(self, chunk, slot, arriving=False):
+        flip, block, half = self.SENDS[slot]
+        ref = self._block(chunk, jnp.bitwise_xor(flip, block) if arriving else block, half)
+        return remote(
+            ref, ref, self.send.at[chunk, slot], self.recv.at[chunk, slot], self.here.plane(flip)
         )
-        put.start()
-        puts.append(put)
-    for t in range(CHUNKS + 4):
-        if t < CHUNKS:
-            gather.begin(t)
-        if 0 <= t - 1 < CHUNKS:
-            gather.relay(t - 1)
-        if 0 <= t - 3 < CHUNKS:
-            gather.share(t - 3)
-        if 0 <= t - 4 < CHUNKS:
-            gather.finish(t - 4)
-    for put in puts:
-        put.wait()
+
+    def begin(self, i):
+        for slot in (0, 1, 2):
+            self._copy(i, slot).start()
+
+    def relay(self, i):
+        self._copy(i, 0, True).wait_recv()
+        self._copy(i, 5).start()
+        self._copy(i, 1, True).wait_recv()
+        self._copy(i, 6).start()
+        self._copy(i, 3).start()
+        self._copy(i, 4).start()
+
+    def share(self, i):
+        self._copy(i, 5, True).wait_recv()
+        self._copy(i, 7).start()
+        self._copy(i, 6, True).wait_recv()
+        self._copy(i, 8).start()
+
+    def finish(self, i):
+        for slot in (2, 3, 4, 7, 8):
+            self._copy(i, slot, True).wait_recv()
+
+    def tick(self, t, prepare):
+        def begin(i):
+            prepare(i)
+            self.begin(i)
+
+        guarded(0, t, CHUNKS, begin)
+        guarded(0, t - 2, CHUNKS, self.relay)
+        guarded(0, t - 3, CHUNKS, self.share)
+        guarded(0, t - 4, CHUNKS, self.finish)
+
+    def drain(self):
+        @pl.loop(0, CHUNKS)
+        def _(i):
+            for slot in range(len(self.SENDS)):
+                self._copy(i, slot).wait_send()
+
+
+class Spread:
+    def __init__(self, here, source, landing, send, recv):
+        self.here, self.source, self.landing = here, source, landing
+        self.send, self.recv = send, recv
+        self.size = source.shape[1] // 2
+
+    def _each(self):
+        here = self.here
+        lats = self.source.shape[0]
+        for j in range(lats):
+            for core in range(2):
+                z = lats * here.c + j
+                own = jnp.logical_and(z == here.z, core == here.c)
+                src = self.source.at[j, pl.ds(core * self.size, self.size), :]
+                peer = (here.d - here.c + core, z)
+                yield own, j * 2 + core, src, peer
+
+    def _land(self, z):
+        return self.landing.at[pl.ds(pl.multiple_of(z * self.size, self.size), self.size), :]
+
+    def start(self):
+        z = self.here.z
+        for own, index, src, peer in self._each():
+
+            @pl.when(own)
+            def _():
+                pltpu.make_async_copy(src, self._land(z), self.recv.at[z]).start()
+
+            @pl.when(jnp.logical_not(own))
+            def _():
+                remote(src, self._land(z), self.send.at[index], self.recv.at[z], peer).start()
+
+    def wait(self):
+        src = self.source.at[0, pl.ds(0, self.size), :]
+        for z in range(4):
+            pltpu.make_async_copy(src, self._land(z), self.recv.at[z]).wait()
+
+    def drain(self):
+        z = self.here.z
+        for own, index, src, peer in self._each():
+
+            @pl.when(jnp.logical_not(own))
+            def _():
+                remote(src, self._land(z), self.send.at[index], self.recv.at[z], peer).wait_send()
+
+
+def gelu_both(v):
+    root = 0.7978845608028654
+    square = v * v
+    t = jnp.tanh(root * (v + 0.044715 * (v * square)))
+    half = 0.5 * (1.0 + t)
+    slope = half + (0.5 * root) * v * (1.0 - t * t) * (1.0 + (3 * 0.044715) * square)
+    return half * v, slope
+
+
+def column_sum(x):
+    return jnp.sum(x, axis=0, keepdims=True)
+
+
+FORWARD_OUTS = (
+    "whole",
+    "xs",
+    "cots",
+    "qkv",
+    "kvo",
+    "att",
+    "lse",
+    "mid",
+    "bra",
+    "nb",
+    "hid",
+    "gph",
+    "bb",
+    "gnb",
+    "vec",
+    "silu",
+    "ups",
+)
+
+
+def forward_kernel(tokens, cot, qkv_w, out_w, up_w, down_w, small, ada, *refs):
+    outs = dict(zip(FORWARD_OUTS, refs))
+    (
+        w,
+        small_all,
+        part,
+        mod_in,
+        mod,
+        vec,
+        silu,
+        xs,
+        ct,
+        na,
+        qkv,
+        kvo,
+        att,
+        lse_acc,
+        lse,
+        mid,
+        bra,
+        nb,
+        gbh,
+        bb,
+        gnb,
+        hid,
+        gph,
+        ups,
+        g_send,
+        g_recv,
+        own_sem,
+        sp_send,
+        sp_recv,
+        sm_send,
+        sm_recv,
+        md_send,
+        md_recv,
+        kv_send,
+        kv_recv,
+        out_sem,
+        ff_sem,
+    ) = refs[len(FORWARD_OUTS) :]
+    here = Place()
+    d, z, c = here.d, here.z, here.c
+    depth, width = qkv_w.shape[0], out_w.shape[1]
+    rows = xs.shape[0]
+    wide = up_w.shape[1]
+    cut = wide // 32
+    tile = 256
+
+    mine = pl.ds(pl.multiple_of(d * depth, depth), depth)
+    for i, k in ((KEYS, 1), (VALUES, 2), (QUERIES, 0)):
+        pltpu.make_async_copy(
+            qkv_w.at[:, pl.ds(k * width, width)], w.at[i, mine, :], own_sem.at[i]
+        ).start()
+    pltpu.make_async_copy(out_w, w.at[OUT, mine, :], own_sem.at[OUT]).start()
+    for j in range(4):
+        for k in range(8):
+            pltpu.make_async_copy(
+                up_w.at[:, pl.ds((4 * k + j) * cut, cut)],
+                w.at[FEED + 2 * j, mine, pl.ds(k * cut, cut)],
+                own_sem.at[FEED + 2 * j],
+            ).start()
+        pltpu.make_async_copy(
+            down_w.at[pl.ds(j * depth, depth), :], w.at[FEED + 2 * j + 1, mine, :], own_sem.at[FEED + 2 * j + 1]
+        ).start()
+
+    def prepare(i):
+        pltpu.make_async_copy(out_w, w.at[i, mine, :], own_sem.at[i]).wait()
+
+    peers = [here.plane(f) for f in range(1, 8)]
+    for core in range(2):
+        for f in range(1, 4):
+            peers.append((d - c + core, jnp.bitwise_xor(z, f)))
+    greet(peers)
+
+    gather = Gather(here, w, g_send, g_recv)
+    tick = functools.partial(gather.tick, prepare=prepare)
+    first = Spread(here, tokens, xs, sp_send.at[0], sp_recv.at[0])
+    second = Spread(here, cot, ct, sp_send.at[1], sp_recv.at[1])
+
+    def small_copy(f):
+        dst = small_all.at[d]
+        return remote(small, dst, sm_send.at[f - 1], sm_recv.at[f - 1], here.plane(f))
+
+    for f in range(1, 8):
+        small_copy(f).start()
+    first.start()
+    tick(0)
+    tick(1)
+    second.start()
+    small_all[d] = small[...]
+    for f in range(1, 8):
+        small_copy(f).wait_recv()
+
+    picked = [
+        small_all[i // 2, pl.ds(16 + 8 * (i % 2) + d, 1), :] for i in range(16)
+    ]
+    cond = jnp.concatenate(picked, axis=0)
+    silu[...] = (cond * jax.nn.sigmoid(cond)).astype(HALF)
+    for i in range(6):
+        product = nn(silu[...], ada[:, pl.ds(i * width, width)])
+        for k in range(8):
+            part[:, 8 * i + k, :] = product[:, k * LANES : (k + 1) * LANES]
+
+    def mod_copy(f):
+        flip = jnp.bitwise_xor(d, f)
+        src = part.at[4 * (flip // 2) + z]
+        return remote(src, mod_in.at[d], md_send.at[f - 1], md_recv.at[f - 1], here.plane(f))
+
+    for f in range(1, 8):
+        mod_copy(f).start()
+    mod_in[d] = part[4 * here.p + z]
+    tick(2)
+    for f in range(1, 8):
+        mod_copy(f).wait_recv()
+    mod[...] = sum(mod_in[k] for k in range(1, 8)) + mod_in[0]
+    for k in range(8):
+        mod[pl.ds(6 * k, 6), :] = mod[pl.ds(6 * k, 6), :] + small_all[k, pl.ds(0, 6), :]
+    for i in range(6):
+        for k in range(8):
+            vec[pl.ds(i, 1), pl.ds(k * LANES, LANES)] = mod[pl.ds(8 * i + k, 1), :]
+    for k in range(8):
+        lanes = pl.ds(k * LANES, LANES)
+        vec[pl.ds(8, 1), lanes] = small_all[k // 2, pl.ds(6 + k % 2, 1), :]
+        vec[pl.ds(9, 1), lanes] = small_all[4 + k // 2, pl.ds(6 + k % 2, 1), :]
+        vec[pl.ds(10, 1), lanes] = small_all[k, pl.ds(8, 1), :]
+        vec[pl.ds(11, 1), lanes] = small_all[k, pl.ds(13, 1), :]
+        for j in range(4):
+            vec[pl.ds(12 + j, 1), lanes] = small_all[k, pl.ds(9 + j, 1), :]
+
+    def row(i):
+        return vec[pl.ds(i, 1), :]
+
+    exits = []
+
+    def leave(src, name, index=None):
+        dst = outs[name] if index is None else outs[name].at[index]
+        copy = pltpu.make_async_copy(src, dst, out_sem.at[len(exits)])
+        copy.start()
+        exits.append(copy)
+
+    leave(vec, "vec")
+    leave(silu, "silu")
+    tick(3)
+    first.wait()
+    leave(xs, "xs")
+
+    block = 128
+
+    @pl.loop(0, rows // block)
+    def _(i):
+        part_rows = pl.ds(pl.multiple_of(i * block, block), block)
+        hat, _ = norm_parts(xs[part_rows, :].astype(F32))
+        na[part_rows, :] = (hat * (1.0 + row(1)) + row(0)).astype(HALF)
+
+    def project(chunk, index, bias):
+        for n in range(width // tile):
+            cols = pl.ds(n * tile, tile)
+            value = nn(na[...], w[chunk, :, cols])
+            if bias is not None:
+                value = value + vec[pl.ds(bias, 1), cols]
+            qkv[index, :, cols] = value.astype(HALF)
+
+    def kv_copy(k):
+        return remote(qkv.at[1 + k], kvo.at[k], kv_send.at[k], kv_recv.at[k], here.plane(1))
+
+    tick(4)
+    leave(w.at[KEYS], "whole", KEYS)
+    project(KEYS, 1, None)
+    kv_copy(0).start()
+    tick(5)
+    leave(w.at[VALUES], "whole", VALUES)
+    project(VALUES, 2, 9)
+    kv_copy(1).start()
+    tick(6)
+    leave(w.at[QUERIES], "whole", QUERIES)
+    project(QUERIES, 0, 8)
+    leave(qkv, "qkv")
+    for k in range(2):
+        kv_copy(k).wait_recv()
+    leave(kvo, "kvo")
+
+    span = 256
+    low = lax.broadcasted_iota(jnp.int32, (span, LANES), 1) < HD
+    lane = lax.broadcasted_iota(jnp.int32, (span, LANES), 1)
+
+    @pl.loop(0, width // LANES)
+    def _(step):
+        cols = pl.ds(pl.multiple_of(step * LANES, LANES), LANES)
+        keys = [qkv[1, :, cols], kvo[0, :, cols]]
+        values = [qkv[2, :, cols], kvo[1, :, cols]]
+        for start in range(0, rows, span):
+            part_rows = pl.ds(start, span)
+            q = qkv[0, part_rows, cols] * HALF(HD**-0.5)
+            pieces = []
+            for head in range(2):
+                own = low if head == 0 else jnp.logical_not(low)
+                qm = jnp.where(own, q, jnp.zeros_like(q))
+                scores = [nt(qm, k) for k in keys]
+                peak = functools.reduce(
+                    jnp.maximum, [jnp.max(s, axis=-1, keepdims=True) for s in scores]
+                )
+                raised = [jnp.exp(s - peak) for s in scores]
+                total = sum(jnp.sum(e, axis=-1, keepdims=True) for e in raised)
+                mixed = sum(nn(e.astype(HALF), v) for e, v in zip(raised, values))
+                pieces.append(mixed / total)
+                logsum = jnp.broadcast_to(peak + jnp.log(total), (span, LANES))
+                lse_acc[part_rows, :] = jnp.where(
+                    lane == 2 * step + head, logsum, lse_acc[part_rows, :]
+                )
+            att[part_rows, cols] = jnp.where(low, pieces[0], pieces[1]).astype(HALF)
+
+        @pl.when(step % 3 == 2)
+        def _():
+            gather.tick(7 + step // 3, prepare)
+
+    lse[...] = lse_acc[...].T
+    leave(lse, "lse")
+    leave(att, "att")
+    leave(w.at[OUT], "whole", OUT)
+    second.wait()
+    leave(ct, "cots")
+
+    for n in range(width // tile):
+        cols = pl.ds(n * tile, tile)
+        branch = nn(att[...], w[OUT, :, cols]) + vec[pl.ds(10, 1), cols]
+        bra[:, cols] = branch.astype(HALF)
+        mid[:, cols] = xs[:, cols].astype(F32) + vec[pl.ds(2, 1), cols] * branch
+    leave(mid, "mid")
+    leave(bra, "bra")
+    tick(9)
+
+    @pl.loop(0, rows // block)
+    def _(i):
+        part_rows = pl.ds(pl.multiple_of(i * block, block), block)
+        hat, _ = norm_parts(mid[part_rows, :])
+        nb[part_rows, :] = (hat * (1.0 + row(4)) + row(3)).astype(HALF)
+        gbh[part_rows, :] = (ct[part_rows, :].astype(F32) * row(5)).astype(HALF)
+        bb[part_rows, :] = jnp.broadcast_to(row(11), (block, width))
+        gnb[part_rows, :] = jnp.zeros((block, width), F32)
+
+    leave(nb, "nb")
+
+    def ff_copies(j, slot):
+        return (
+            pltpu.make_async_copy(hid.at[slot], outs["hid"].at[j], ff_sem.at[0, slot]),
+            pltpu.make_async_copy(gph.at[slot], outs["gph"].at[j], ff_sem.at[1, slot]),
+        )
+
+    @pl.loop(0, 4)
+    def _(j):
+        slot = j % 2
+        up, down = FEED + 2 * j, FEED + 2 * j + 1
+
+        @pl.when(j >= 2)
+        def _():
+            for copy in ff_copies(j, slot):
+                copy.wait()
+
+        for n in range(width // tile):
+            cols = pl.ds(n * tile, tile)
+            pre = nn(nb[...], w[up, :, cols]) + vec[pl.ds(12 + j, 1), cols]
+            grad = nt(gbh[...], w[down, cols, :])
+            value, slope = gelu_both(pre)
+            grad = grad * slope
+            ups[pl.ds(j, 1), cols] = column_sum(grad)
+            hid[slot, :, cols] = value.astype(HALF)
+            gph[slot, :, cols] = grad.astype(HALF)
+        for copy in ff_copies(j, slot):
+            copy.start()
+        gather.tick(10 + 2 * j, prepare)
+        for n in range(width // tile):
+            cols = pl.ds(n * tile, tile)
+            bb[:, cols] = bb[:, cols] + nn(hid[slot], w[down, :, cols])
+            gnb[:, cols] = gnb[:, cols] + nt(gph[slot], w[up, cols, :])
+        gather.tick(11 + 2 * j, prepare)
+
+    leave(bb, "bb")
+    leave(gnb, "gnb")
+    leave(ups, "ups")
+    for slot in range(2):
+        for copy in ff_copies(slot, slot):
+            copy.wait()
+    for copy in exits:
+        copy.wait()
     gather.drain()
-
-
-def gather_all(local):
-    depth, cols = local.shape[1:]
-    return pl.pallas_call(
-        gather_kernel,
-        out_shape=jax.ShapeDtypeStruct((CHUNKS, 8 * depth, cols), HALF),
-        in_specs=[pl.BlockSpec(memory_space=pltpu.VMEM)],
-        out_specs=pl.BlockSpec(memory_space=pl.ANY),
-        scratch_shapes=[
-            pltpu.SemaphoreType.DMA((CHUNKS, Gather.SLOTS)),
-            pltpu.SemaphoreType.DMA((CHUNKS, Gather.SLOTS)),
-            pltpu.SemaphoreType.DMA((CHUNKS,)),
-        ],
+    first.drain()
+    second.drain()
+    for f in range(1, 8):
+        small_copy(f).wait_send()
+        mod_copy(f).wait_send()
+    for k in range(2):
+        kv_copy(k).wait_send()
+
+
+def forward(tokens, cot, qkv_w, out_w, up_w, down_w, small, ada):
+    depth, width = qkv_w.shape[0], out_w.shape[1]
+    rows = tokens.shape[0] * tokens.shape[1]
+    sds = jax.ShapeDtypeStruct
+    flat, real = sds((rows, width), HALF), sds((rows, width), F32)
+    shapes = dict(
+        whole=sds((4, width, width), HALF),
+        xs=flat,
+        cots=flat,
+        qkv=sds((3, rows, width), HALF),
+        kvo=sds((2, rows, width), HALF),
+        att=flat,
+        lse=sds((LANES, rows), F32),
+        mid=real,
+        bra=flat,
+        nb=flat,
+        hid=sds((4, rows, width), HALF),
+        gph=sds((4, rows, width), HALF),
+        bb=real,
+        gnb=real,
+        vec=sds((16, width), F32),
+        silu=sds((16, LANES), HALF),
+        ups=sds((8, width), F32),
+    )
+    hbm = pl.BlockSpec(memory_space=pl.ANY)
+    vmem = pl.BlockSpec(memory_space=pltpu.VMEM)
+    dma = pltpu.SemaphoreType.DMA
+    half = lambda *s: pltpu.VMEM(s, HALF)
+    full = lambda *s: pltpu.VMEM(s, F32)
+    scratch = [
+        half(CHUNKS, width, width),
+        full(8, 32, LANES),
+        full(16, 48, LANES),
+        full(8, 48, LANES),
+        full(48, LANES),
+        full(16, width),
+        half(16, LANES),
+        half(rows, width),
+        half(rows, width),
+        half(rows, width),
+        half(3, rows, width),
+        half(2, rows, width),
+        half(rows, width),
+        full(rows, LANES),
+        full(LANES, rows),
+        full(rows, width),
+        half(rows, width),
+        half(rows, width),
+        half(rows, width),
+        full(rows, width),
+        full(rows, width),
+        half(2, rows, width),
+        half(2, rows, width),
+        full(8, width),
+        dma((CHUNKS, 9)),
+        dma((CHUNKS, 9)),
+        dma((CHUNKS,)),
+        dma((2, 4)),
+        dma((2, 4)),
+        dma((7,)),
+        dma((7,)),
+        dma((7,)),
+        dma((7,)),
+        dma((2,)),
+        dma((2,)),
+        dma((24,)),
+        dma((2, 2)),
+    ]
+    got = pl.pallas_call(
+        forward_kernel,
+        out_shape=tuple(shapes[name] for name in FORWARD_OUTS),
+        in_specs=[hbm] * 6 + [vmem] * 2,
+        out_specs=(hbm,) * len(FORWARD_OUTS),
+        scratch_shapes=scratch,
         compiler_params=pltpu.CompilerParams(
-            collective_id=1, has_side_effects=True, vmem_limit_bytes=32 << 20
+            collective_id=1, has_side_effects=True, vmem_limit_bytes=67043328
         ),
-        name="gather_all",
-    )(local)
+        name="forward",
+    )(tokens, cot, qkv_w, out_w, up_w, down_w, small, ada)
+    return dict(zip(FORWARD_OUTS, got))
 
 
 class Reduce:
@@ -338,6 +807,8 @@
                 self.own[slot, k].astype(F32) + self.rc[i, k].astype(F32)
             ).astype(HALF)
 
+        for other_y in range(2):
+            pass
         self._remote(
             i, 1, self.s.at[slot].reshape(2, 2, self.depth, self.cols).at[:, 1 - self.x, :, pl.ds(0, half)],
             self.rx.at[i], self._plane(2),
@@ -479,27 +950,7 @@
     )(grads)
 
 
-def norm_parts(rows):
-    centred = rows - jnp.mean(rows, axis=-1, keepdims=True)
-    variance = jnp.mean(centred * centred, axis=-1, keepdims=True)
-    inverse = lax.rsqrt(variance + EPSILON)
-    return centred * inverse, inverse
-
-
-def norm_grad(grad, hat, inverse, scale):
-    g = grad * (1.0 + scale)
-    return (
-        g
-        - jnp.mean(g, axis=-1, keepdims=True)
-        - hat * jnp.mean(g * hat, axis=-1, keepdims=True)
-    ) * inverse
-
-
-def gelu_tanh(inputs):
-    return jax.nn.gelu(inputs, approximate=True)
-
-
-def body(
+def body_any(
     tokens,
     condition,
     ada_weight,
@@ -581,30 +1032,10 @@
     modulation = (modulation + ada_bias_full).reshape(6, 1, width)
     shift_a, scale_a, gate_a, shift_b, scale_b, gate_b = [modulation[i] for i in range(6)]
 
-    own = dp == 8 and seq == 4 and lats == 2
-    wide = up_bias.shape[0] * dp
-    if own:
-        cut = wide // (4 * dp)
-        local = jnp.concatenate(
-            [
-                qkv_weight.reshape(depth, 3, width).transpose(1, 0, 2),
-                out_weight[None],
-                up_weight.reshape(depth, dp, 4, cut).transpose(2, 0, 1, 3).reshape(4, depth, width),
-                down_weight.reshape(4, cut, width),
-            ],
-            axis=0,
-        )
-        whole = gather_all(local)
-        qkv_full = whole[:3].transpose(1, 0, 2).reshape(width, 3 * width)
-        out_full = whole[3]
-        up_full = whole[4:8].transpose(1, 0, 2).reshape(width, wide)
-        down_full = whole[8:].reshape(wide, width)
-        up_bias_full = up_bias_full.reshape(dp, 4, cut).transpose(1, 0, 2).reshape(-1)
-    else:
-        qkv_full = lax.all_gather(qkv_weight, "dp", axis=0, tiled=True)
-        out_full = lax.all_gather(out_weight, "dp", axis=0, tiled=True)
-        up_full = lax.all_gather(up_weight, "dp", axis=0, tiled=True)
-        down_full = lax.all_gather(down_weight, "dp", axis=0, tiled=True)
+    qkv_full = lax.all_gather(qkv_weight, "dp", axis=0, tiled=True)
+    out_full = lax.all_gather(out_weight, "dp", axis=0, tiled=True)
+    up_full = lax.all_gather(up_weight, "dp", axis=0, tiled=True)
+    down_full = lax.all_gather(down_weight, "dp", axis=0, tiled=True)
 
     rows = spread(tokens).astype(F32)
     cot = spread(cotangent).astype(F32)
@@ -698,27 +1129,6 @@
         share = lax.psum_scatter(grad, "dp", scatter_dimension=0, tiled=True)
         return lax.psum(share, "seq").astype(F32)
 
-    if own:
-        up_bias_grad = up_bias_grad.reshape(4, dp, cut).transpose(1, 0, 2).reshape(-1)
-        grads = jnp.concatenate(
-            [
-                qkv_weight_grad.reshape(width, 3, width).transpose(1, 0, 2),
-                out_weight_grad[None],
-                up_weight_grad.reshape(width, 4, width).transpose(1, 0, 2),
-                down_weight_grad.reshape(4, width, width),
-            ],
-            axis=0,
-        )
-        shares = reduce_all(grads.reshape(CHUNKS, dp // 2, 2, depth, width)).astype(F32)
-        qkv_g = shares[:3].transpose(1, 0, 2).reshape(depth, 3 * width)
-        out_g = shares[3]
-        up_g = shares[4:8].reshape(4, depth, dp, cut).transpose(1, 2, 0, 3).reshape(depth, wide)
-        down_g = shares[8:].reshape(4 * cut, width)
-    else:
-        qkv_g, out_g, up_g, down_g = map(
-            reduce_weight, (qkv_weight_grad, out_weight_grad, up_weight_grad, down_weight_grad)
-        )
-
     bias_parts = jnp.concatenate(
         [
             b.reshape(dp, -1)
@@ -729,6 +1139,186 @@
     bias_parts = lax.psum_scatter(bias_parts, "dp", scatter_dimension=0, tiled=True)
     bias_parts = lax.psum(bias_parts, "seq")[0]
     cuts = [c - sizes[0] for c in cuts[1:]]
+    qv_g, ob_g, ub_g, db_g = [bias_parts[a:b] for a, b in zip(cuts[:-1], cuts[1:])]
+    return (
+        output,
+        tokens_grad,
+        condition_grad,
+        ada_weight_grad,
+        ada_bias_grad,
+        reduce_weight(qkv_weight_grad),
+        qv_g,
+        reduce_weight(out_weight_grad),
+        ob_g,
+        reduce_weight(up_weight_grad),
+        ub_g,
+        reduce_weight(down_weight_grad),
+        db_g,
+    )
+
+
+def body(
+    tokens,
+    condition,
+    ada_weight,
+    ada_bias,
+    qkv_weight,
+    qv_bias,
+    out_weight,
+    out_bias,
+    up_weight,
+    up_bias,
+    down_weight,
+    down_bias,
+    cotangent,
+):
+    lats, part, width = tokens.shape
+    dp = lax.axis_size("dp")
+    seq = lax.axis_size("seq")
+    if (dp, seq, lats) != (8, 4, 2):
+        return body_any(
+            tokens,
+            condition,
+            ada_weight,
+            ada_bias,
+            qkv_weight,
+            qv_bias,
+            out_weight,
+            out_bias,
+            up_weight,
+            up_bias,
+            down_weight,
+            down_bias,
+            cotangent,
+        )
+    me = lax.axis_index("dp")
+    z = lax.axis_index("seq")
+    core = me % 2
+    first = core == 0
+    depth = ada_weight.shape[0]
+    wide = dp * up_bias.shape[0]
+    cut = wide // (4 * dp)
+
+    def flip(x):
+        return lax.ppermute(x, "dp", [(i, i ^ 1) for i in range(dp)])
+
+    def collect(x):
+        both = x.reshape(seq, part // 2, width)
+        both = lax.all_to_all(both, "seq", 0, 0, tiled=True)
+        both = both.reshape(2, lats, part // 2, width)
+        mine = lax.dynamic_index_in_dim(both, core, 0, keepdims=False)
+        give = lax.dynamic_index_in_dim(both, 1 - core, 0, keepdims=False)
+        got = flip(give)
+        return jnp.stack(
+            [jnp.where(first, mine, got), jnp.where(first, got, mine)], axis=1
+        ).reshape(lats, part, width)
+
+    small = jnp.concatenate(
+        [
+            ada_bias.reshape(-1, LANES),
+            qv_bias.reshape(-1, LANES),
+            out_bias.reshape(-1, LANES),
+            up_bias.reshape(-1, LANES),
+            down_bias.reshape(-1, LANES),
+            jnp.zeros((2, LANES), HALF),
+            condition.reshape(-1, LANES),
+        ],
+        axis=0,
+    ).astype(F32)
+    f = forward(
+        tokens, cotangent, qkv_weight, out_weight, up_weight, down_weight, small, ada_weight
+    )
+    whole = f["whole"]
+    vec = f["vec"]
+    shift_a, scale_a, gate_a, shift_b, scale_b, gate_b = [vec[i : i + 1] for i in range(6)]
+    cot = f["cots"].astype(F32)
+    middle = f["mid"]
+    branch_b = f["bb"]
+    output = collect((middle + gate_b * branch_b).astype(HALF))
+    grad_gate_b = jnp.sum(cot * branch_b, axis=0)
+    grad_branch_b = cot * gate_b
+    down_bias_grad = jnp.sum(grad_branch_b, axis=0)
+    gbh = grad_branch_b.astype(HALF)
+    chunks = [None] * CHUNKS
+    for j in range(4):
+        chunks[FEED + 2 * j] = tn(f["nb"], f["gph"][j]).astype(HALF)
+        chunks[FEED + 2 * j + 1] = tn(f["hid"][j], gbh).astype(HALF)
+    up_bias_grad = f["ups"][:4].reshape(4, dp, cut).transpose(1, 0, 2).reshape(-1)
+    hat_b, inverse_b = norm_parts(middle)
+    gnb = f["gnb"]
+    branch_a = f["bra"].astype(F32)
+    grad_shift_b = jnp.sum(gnb, axis=0)
+    grad_scale_b = jnp.sum(gnb * hat_b, axis=0)
+    grad_middle = cot + norm_grad(gnb, hat_b, inverse_b, scale_b)
+    grad_gate_a = jnp.sum(grad_middle * branch_a, axis=0)
+    grad_branch_a = grad_middle * gate_a
+    out_bias_grad = jnp.sum(grad_branch_a, axis=0)
+    gbah = grad_branch_a.astype(HALF)
+    chunks[OUT] = tn(f["att"], gbah).astype(HALF)
+    grad_attended = nt(gbah, whole[OUT]).astype(HALF)
+    projected = f["qkv"].transpose(1, 0, 2).reshape(-1, 3 * width)
+    other = f["kvo"].transpose(1, 0, 2).reshape(-1, 2 * width)
+    grad_q, dk, dko, dv, dvo = attend_grad(
+        projected, [other], grad_attended, f["att"], f["lse"], width
+    )
+    grad_k = (dk.astype(F32) + flip(dko).astype(F32)).astype(HALF)
+    grad_v = (dv.astype(F32) + flip(dvo).astype(F32)).astype(HALF)
+    rows = f["xs"].astype(F32)
+    hat_a, inverse_a = norm_parts(rows)
+    normed_a = (hat_a * (1.0 + scale_a) + shift_a).astype(HALF)
+    chunks[KEYS] = tn(normed_a, grad_k).astype(HALF)
+    chunks[VALUES] = tn(normed_a, grad_v).astype(HALF)
+    chunks[QUERIES] = tn(normed_a, grad_q).astype(HALF)
+    qv_bias_grad = jnp.concatenate(
+        [jnp.sum(grad_q.astype(F32), axis=0), jnp.sum(grad_v.astype(F32), axis=0)]
+    )
+    grad_normed_a = (
+        nt(grad_q, whole[QUERIES]) + nt(grad_k, whole[KEYS]) + nt(grad_v, whole[VALUES])
+    )
+    grad_shift_a = jnp.sum(grad_normed_a, axis=0)
+    grad_scale_a = jnp.sum(grad_normed_a * hat_a, axis=0)
+    grad_tokens = grad_middle + norm_grad(grad_normed_a, hat_a, inverse_a, scale_a)
+    tokens_grad = collect(grad_tokens.astype(HALF)).astype(F32)
+    grads = jnp.stack(chunks).reshape(CHUNKS, dp // 2, 2, depth, width)
+    shares = reduce_all(grads).astype(F32)
+    qkv_g = jnp.concatenate([shares[QUERIES], shares[KEYS], shares[VALUES]], axis=1)
+    out_g = shares[OUT]
+    up_g = shares[FEED::2].reshape(4, depth, dp, cut).transpose(1, 2, 0, 3).reshape(depth, wide)
+    down_g = shares[FEED + 1 :: 2].reshape(4 * cut, width)
+
+    grad_mod = jnp.concatenate(
+        [grad_shift_a, grad_scale_a, grad_gate_a, grad_shift_b, grad_scale_b, grad_gate_b]
+    )
+    every = lax.all_gather(grad_mod, "seq", axis=0, tiled=False)
+    every = lax.all_gather(every, "dp", axis=0, tiled=False)
+    every = every.reshape(dp // 2, 2, seq, 6 * width).sum(axis=1)
+    every = every.reshape(dp * lats, 6 * width)
+    every_half = every.astype(HALF)
+    ada_weight_grad = tn(f["silu"], every_half)
+    bias_len = ada_bias.shape[0]
+    ada_bias_grad = jnp.sum(
+        lax.dynamic_slice_in_dim(every, me * bias_len, bias_len, axis=1), axis=0
+    )
+    cond_part = nt(every_half, ada_weight).reshape(dp, lats, depth)
+    cond_part = lax.all_to_all(cond_part, "dp", 0, 0, tiled=True)
+    cond_part = cond_part.transpose(1, 0, 2).reshape(lats, width)
+    cond_float = condition.astype(F32)
+    sigmoid_cond = jax.nn.sigmoid(cond_float)
+    silu_slope = sigmoid_cond * (1.0 + cond_float * (1.0 - sigmoid_cond))
+    condition_grad = silu_slope * cond_part
+    bias_parts = jnp.concatenate(
+        [
+            b.reshape(dp, -1)
+            for b in (qv_bias_grad, out_bias_grad, up_bias_grad, down_bias_grad)
+        ],
+        axis=1,
+    )
+    bias_parts = lax.psum_scatter(bias_parts, "dp", scatter_dimension=0, tiled=True)
+    bias_parts = lax.psum(bias_parts, "seq")[0]
+    sizes = [a.shape[0] for a in (qv_bias, out_bias, up_bias, down_bias)]
+    cuts = [0]
+    for size in sizes:
+        cuts.append(cuts[-1] + size)
     qv_g, ob_g, ub_g, db_g = [bias_parts[a:b] for a, b in zip(cuts[:-1], cuts[1:])]
     return (
         output,

time: 736 us -> 557 us (0.76)
  local copies, waits for them, and re-layouts: 127 us -> 59.5 us
  matrix products: 97.2 us -> 54.4 us
  other arithmetic: 55.5 us -> 27.1 us
  between operations: 15 us -> 1.62 us
  starting transfers between devices: 24.3 us -> 13.2 us
  blocking collectives: 70.1 us -> 60 us
    transpose x9 -> x3, local copies, waits for them, and re-layouts: 53.8 us -> 4.68 us  [the longest x1 3.19 us: body(): projected = f['qkv'].transpose(1, 0, 2).reshape(-1, 3 * width)]
    dot_general x5 -> x0, matrix products: 31.6 us -> none  [nn(): return jnp.dot(a, b, preferred_element_type=F32)]
    all_to_all x2 -> x0, waiting for transfers between devices: 24.2 us -> none  [spread(): return lax.all_to_all(both, 'seq', 0, 0, tiled=True).reshape(-1, width)]
    dot_general x5, matrix products: 38.5 us -> 15.4 us  [nt(): lax.dot_general(a, b, (((1,), (1,)), ((), ())), preferred_element_type=F32)]
    concatenate x6 -> x1, other arithmetic: 23.1 us -> 1.25 us  [body(): jnp.concatenate([shares[QUERIES], shares[KEYS], shares[VALUES]], axis=1)]
    all_to_all x2, waiting for transfers between devices: 0.01 us -> 14.4 us  [collect(): both = lax.all_to_all(both, 'seq', 0, 0, tiled=True)]
    reshape x8 -> x4, local copies, waits for them, and re-layouts: 21.4 us -> 8.88 us  [the longest x1 3.3 us: body(): other = f['kvo'].transpose(1, 0, 2).reshape(-1, 2 * width)]
    dot_general x5 -> x13, matrix products: 27.1 us -> 38.9 us  [tn(): lax.dot_general(a, b, (((0,), (0,)), ((), ())), preferred_element_type=F32)]
  transfers between devices with their start and end apart: 12 -> 7, of which waited for: 1 -> 2; matrix products, arithmetic and copies ran while one was open for 27% -> 21% of each run, Pallas kernels for 41% -> 33%
where the time goes in v3:
time: 557 us; the launch traced here: 547 us
  Pallas kernels  313 us (56%)
  blocking collectives  60 us (11%)
  local copies, waits for them, and re-layouts  59.5 us (11%)
  matrix products  54.4 us (10%)
  other arithmetic  27.1 us (5%)
  waiting for transfers between devices  18.5 us (3%)
  starting transfers between devices  13.2 us (2%)
    pallas_call x1, Pallas kernels, reduce_all(): pl.pallas_call(reduce_kernel, out_shape=jax.ShapeDtypeStruct((CHUNKS, dep...  147 us
    pallas_call x1, Pallas kernels, forward(): pl.pallas_call(forward_kernel, out_shape=tuple((shapes[name] for name in...  130 us
    dot_general x13, matrix products, tn(): lax.dot_general(a, b, (((0,), (0,)), ((), ())), preferred_element_type=F32)  38.9 us
    pallas_call x1, Pallas kernels, attend_grad(): pl.pallas_call(functools.partial(attend_grad_kernel, groups), grid=(tiles...  36.2 us
    unnamed x126, local copies, waits for them, and re-layouts  31.2 us
    unnamed x1, blocking collectives  24.2 us
    dot_general x5, matrix products, nt(): lax.dot_general(a, b, (((1,), (1,)), ((), ())), preferred_element_type=F32)  15.4 us
    all_to_all x2, waiting for transfers between devices, collect(): both = lax.all_to_all(both, 'seq', 0, 0, tiled=True)  14.4 us
  transfers between devices with their start and end apart: 7, of which 2 were waited for; matrix products, arithmetic and copies ran while one was open for 21% of the time, Pallas kernels for 33%

profile of v3, /device:TPU:0, one launch (start us, length us, event | category | flops | bytes accessed | tf_op | source)
XLA Modules:
  0.0 547.3 jit_solution(6789136166762781968)
XLA Ops:
  3.4 130.2 %forward.1 = (bf16[4,1024,1024]{2,1,0:T(8,128)(2,1)}, bf16[512,1024]{1,0:T(8,128)(2,1)}, bf16[512,1024]{1,0:T(8,128)(2,1)}, bf16[3,512,1024]{2,1,0:T(8,128)(2,1)...) custom-call(bf16[2,256,1024]{2,1,0:T(8,128)(2,1)} %tokens.1, ...), custom_call_target="tpu_custom_call" | custom-call | tf_op jit(solution)/shard_map/forward/pallas_call | solution.py:735
  140.2 3.9 fusion.6
  144.1 4.2 all-to-all-start
  148.3 3.2 copy.41
  151.5 3.0 copy.43.refs_0_.refs_1_.refs_3_
  154.6 3.3 copy.50
  157.9 3.9 fusion.34.refs_5_
  161.8 36.2 %attend_grad.1 = (bf16[512,1024]{1,0:T(8,128)(2,1)S(1)}, bf16[512,1024]{1,0:T(8,128)(2,1)S(1)}, bf16[512,1024]{1,0:T(8,128)(2,1)}, bf16[512,1024]{1,0:T(8,128)(2,1)S(1)}, bf16[512,1024]{1,0:T(8,128)(2,1)}) custom-call(bf16[512,3072]{1,0:T(8,128)(2,1)} %copy.43.refs_0_.refs_1_.refs_3_, bf16[512,3072]{1,0:T(8,128)(2,1)} %copy.43.refs_0_.refs_1_.refs_3_, ...), custom_call_target="tpu_custom_call" | custom-call | tf_op jit(solution)/shard_map/attend_grad/pallas_call | solution.py:138
  198.6 4.3 convolution_convert_fusion.7
  202.9 2.7 convolution_convert_fusion.5
  206.0 2.7 convolution_convert_fusion.6
  208.6 2.6 convolution_convert_fusion.4
  211.3 2.6 convolution_convert_fusion.3
  213.9 2.7 convolution_convert_fusion.2
  216.6 2.6 convolution_convert_fusion
  223.7 4.1 convolution_convert_fusion.9
  227.9 2.6 convolution_convert_fusion.8
  230.5 4.3 convolution_convert_fusion.1
  238.8 5.0 fusion.13
  243.8 13.7 %all-gather = f32[24576]{0:T(1024)S(1)} all-gather(f32[6144]{0:T(1024)S(1)} %constant_dynamic-update-slice_fusion.13), channel_id=2, replica_groups=mesh['dp'=8,'seq'=4] {'seq'}, dimensions={0}, use_global_device_ids=true | all-gather | bytes 122880 | tf_op jit(solution)/shard_map/all_gather | solution.py:1292
  257.6 10.2 %all-gather.2 = f32[8,4,6144]{2,1,0:T(4,128)S(1)} all-gather(f32[1,4,6144]{2,1,0:T(4,128)S(1)} %reshape.197), channel_id=3, replica_groups=mesh['dp'=8,'seq'=4] {'dp'}, dimensions={0}, use_global_device_ids=true | all-gather | bytes 884736 | tf_op jit(solution)/shard_map/all_gather | solution.py:1293
  270.5 2.6 fusion.30
  273.1 2.7 convolution_convert_fusion.11
  279.0 24.2 %all-reduce = f32[8,1024]{1,0:T(8,128)} all-reduce(f32[8,1024]{1,0:T(8,128)S(1)} %pad_maximum_fusion.3), channel_id=4, replica_groups=mesh['dp'=8,'seq'=4] {'dp'}, use_global_device_ids=true, to_apply=%region_20.21.clone | all-reduce | flops 8192 | bytes 65536
  303.2 2.7 convolution_convert_fusion.10
  328.4 11.8 %psum.7 = f32[1,1024]{1,0:T(1,128)S(1)} all-reduce(f32[1,1024]{1,0:T(1,128)S(1)} %constant_dynamic-slice_fusion), channel_id=1, replica_groups=mesh['dp'=8,'seq'=4] {'seq'}, use_global_device_ids=true, to_apply=%region_21.22 | all-reduce | flops 1024 | bytes 8192 | tf_op jit(solution)/shard_map/psum | solution.py:1317
  345.9 146.5 %reduce_all.1 = bf16[12,128,1024]{2,1,0:T(8,128)(2,1)} custom-call(bf16[12,4,2,128,1024]{4,3,2,1,0:T(8,128)(2,1)} %constant_dynamic-update-slice_fusion.1.grads), custom_call_target="tpu_custom_call" | custom-call | tf_op jit(solution)/shard_map/reduce_all/pallas_call | solution.py:940
  492.5 5.5 %convert_element_type.145 = f32[12,128,1024]{2,1,0:T(8,128)} convert(bf16[12,128,1024]{2,1,0:T(8,128)(2,1)} %reduce_all.1) | non-fusion elementwise | flops 1572864 | bytes 9437184 | tf_op jit(solution)/shard_map/convert_element_type | solution.py:1283
  503.6 4.5 all-to-all-start.1
  519.8 14.4 %all-to-all-done.1 = bf16[4,128,1024]{2,1,0:T(8,128)(2,1)S(1)} async-done(((bf16[4,128,1024]{2,1,0:T(8,128)(2,1)}), bf16[4,128,1024]{2,1,0:T(8,128)(2,1)S(1)}, u32[]{:S(2)}, u32[]{:S(2)}) %all-to-all-start.1) | async-done | bytes 1048608 | tf_op jit(solution)/shard_map/all_to_all | solution.py:1207
  534.1 3.3 all-to-all-start.2
  538.0 4.1 all-to-all-done.2
  (188 shorter events, 74.9 us)
Async XLA Ops:
  133.6 2.8 copy-start.2
  134.6 89.1 %copy-start.40 = (f32[1,1024]{1,0:T(1,128)}, f32[1,1024]{1,0:T(1,128)S(1)}, u32[]{:S(2)}) copy-start(f32[1,1024]{1,0:T(1,128)S(1)} %get-tuple-element.84) | copy-start | bytes 12292
  134.6 104.2 %copy-start.33 = (f32[1,1024]{1,0:T(1,128)}, f32[1,1024]{1,0:T(1,128)S(1)}, u32[]{:S(2)}) copy-start(f32[1,1024]{1,0:T(1,128)S(1)} %get-tuple-element.85) | copy-start | bytes 12292
  144.1 359.5 %all-to-all-start = ((bf16[4,128,1024]{2,1,0:T(8,128)(2,1)}), bf16[4,128,1024]{2,1,0:T(8,128)(2,1)}, u32[]{:S(2)}, u32[]{:S(2)}) async-start(bf16[4,128,1024]{2,1,0:T(8,128)(2,1)} %bitcast.6), calls=%async_computation | async-start | bytes 2097152 | tf_op jit(solution)/shard_map/all_to_all | solution.py:1207
  154.6 3.3 copy-start.5
  157.9 3.9 copy-start
  198.0 40.8 %collective-permute-start.2 = (bf16[512,1024]{1,0:T(8,128)(2,1)}, bf16[512,1024]{1,0:T(8,128)(2,1)}, u32[]{:S(2)}, u32[]{:S(2)}) collective-permute-start(bf16[512,1024]{1,0:T(8,128)(2,1)} %get-tuple-element.49), channel_id=1, source_target_pairs={{0,4},{4,0},{8,12},{12,8},{16,20},{20,16},{24,28},{28,24},{1,5},{5... | collective-permute-start | bytes 3145736 | tf_op jit(solution)/shard_map/ppermute | solution.py:1203
  198.1 38.1 %collective-permute-start.1 = (bf16[512,1024]{1,0:T(8,128)(2,1)}, bf16[512,1024]{1,0:T(8,128)(2,1)}, u32[]{:S(2)}, u32[]{:S(2)}) collective-permute-start(bf16[512,1024]{1,0:T(8,128)(2,1)} %get-tuple-element.47), channel_id=1, source_target_pairs={{0,4},{4,0},{8,12},{12,8},{16,20},{20,16},{24,28},{28,24},{1,5},{5... | collective-permute-start | bytes 3145736 | tf_op jit(solution)/shard_map/ppermute | solution.py:1203
  198.6 4.3 copy-start.45
  198.6 4.3 copy-start.47
  202.9 2.7 copy-start.22
  202.9 3.1 copy-start.46
  219.2 3.1 copy-start.39
  219.2 3.9 copy-start.49
  220.6 18.2 %copy-start.26 = (f32[512]{0:T(512)}, f32[512]{0:T(512)S(1)}, u32[]{:S(2)}) copy-start(f32[512]{0:T(512)S(1)} %broadcast_multiply_fusion.1) | copy-start | bytes 6148
  222.3 16.5 %copy-start.36 = (f32[512]{0:T(512)}, f32[512]{0:T(512)S(1)}, u32[]{:S(2)}) copy-start(f32[512]{0:T(512)S(1)} %add_rsqrt_fusion) | copy-start | bytes 6148
  223.7 4.1 copy-start.6
  223.7 4.1 copy-start.24
  227.9 7.0 %slice-start = ((s8[8388608]{0:T(1024)(128)(4,1)}), s8[4194304]{0:T(1024)(128)(4,1)S(1)}, s32[]{:S(2)}) async-start(s8[8388608]{0:T(1024)(128)(4,1)} %bitcast.210), calls=%async_computation.3 | async-start | bytes 8388608
  230.5 4.4 slice-start.1
  277.3 25.9 %copy-start.27 = (f32[512]{0:T(512)S(1)}, f32[512]{0:T(512)}, u32[]{:S(2)}) copy-start(f32[512]{0:T(512)} %copy-done.26) | copy-start | bytes 6148
  277.3 25.9 %copy-start.34 = (f32[1,1024]{1,0:T(1,128)S(1)}, f32[1,1024]{1,0:T(1,128)}, u32[]{:S(2)}) copy-start(f32[1,1024]{1,0:T(1,128)} %copy-done.33) | copy-start | bytes 12292
  277.3 25.9 %copy-start.37 = (f32[512]{0:T(512)S(1)}, f32[512]{0:T(512)}, u32[]{:S(2)}) copy-start(f32[512]{0:T(512)} %copy-done.36) | copy-start | bytes 6148
  277.4 25.9 %copy-start.41 = (f32[1,1024]{1,0:T(1,128)S(1)}, f32[1,1024]{1,0:T(1,128)}, u32[]{:S(2)}) copy-start(f32[1,1024]{1,0:T(1,128)} %copy-done.40) | copy-start | bytes 12292
  324.7 16.8 %copy-start.25 = (f32[8,2,128]{2,0,1:T(8,128)S(1)}, f32[8,2,128]{2,0,1:T(8,128)}, u32[]{:S(2)}) copy-start(f32[8,2,128]{2,0,1:T(8,128)} %fusion.30) | copy-start | bytes 24580
  324.7 17.4 %copy-start.16 = (bf16[1024,1024]{1,0:T(8,128)(2,1)S(1)}, bf16[1024,1024]{1,0:T(8,128)(2,1)}, u32[]{:S(2)}) copy-start(bf16[1024,1024]{1,0:T(8,128)(2,1)} %convolution_convert_fusion.1) | copy-start | bytes 6291460
  492.5 5.5 %copy-start.1 = (bf16[12,128,1024]{2,1,0:T(8,128)(2,1)S(1)}, bf16[12,128,1024]{2,1,0:T(8,128)(2,1)}, u32[]{:S(2)}) copy-start(bf16[12,128,1024]{2,1,0:T(8,128)(2,1)} %reduce_all.1) | copy-start | bytes 9437188
  503.6 30.5 %all-to-all-start.1 = ((bf16[4,128,1024]{2,1,0:T(8,128)(2,1)}), bf16[4,128,1024]{2,1,0:T(8,128)(2,1)S(1)}, u32[]{:S(2)}, u32[]{:S(2)}) async-start(bf16[4,128,1024]{2,1,0:T(8,128)(2,1)} %bitcast.165), calls=%async_computation.1 | async-start | bytes 2097152 | tf_op jit(solution)/shard_map/all_to_all | solution.py:1207
  516.8 25.3 %copy-start.31 = (bf16[2,1024]{1,0:T(2,128)(2,1)S(1)}, bf16[2,1024]{1,0:T(2,128)(2,1)}, u32[]{:S(2)}) copy-start(bf16[2,1024]{1,0:T(2,128)(2,1)} %param.14) | copy-start | bytes 12292
  519.2 23.6 %collective-permute-start = (bf16[2,128,1024]{2,1,0:T(8,128)(2,1)S(1)}, bf16[2,128,1024]{2,1,0:T(8,128)(2,1)S(1)}, u32[]{:S(2)}, u32[]{:S(2)}) collective-permute-start(bf16[2,128,1024]{2,1,0:T(8,128)(2,1)S(1)} %dynamic-slice_bitcast_fusion.1), channel_id=1, source_target_pairs={{0,4},{4,0},{8,12},{12,8},{16,20},{20,16},{24,28},{28,24},{1,5},{5... | collective-permute-start | bytes 1572872 | tf_op jit(solution)/shard_map/ppermute | solution.py:1203
  534.1 8.0 %all-to-all-start.2 = ((f32[8,2,128]{2,1,0:T(2,128)}), f32[8,2,128]{2,1,0:T(2,128)S(1)}, u32[]{:S(2)}, u32[]{:S(2)}) async-start(f32[8,2,128]{2,1,0:T(2,128)} %copy.48), calls=%async_computation.2 | async-start | bytes 16384 | tf_op jit(solution)/shard_map/all_to_all | solution.py:1303
  537.5 7.5 %collective-permute-start.3 = (bf16[2,128,1024]{2,1,0:T(8,128)(2,1)S(1)}, bf16[2,128,1024]{2,1,0:T(8,128)(2,1)S(1)}, u32[]{:S(2)}, u32[]{:S(2)}) collective-permute-start(bf16[2,128,1024]{2,1,0:T(8,128)(2,1)S(1)} %dynamic-slice_bitcast_fusion), channel_id=1, source_target_pairs={{0,4},{4,0},{8,12},{12,8},{16,20},{20,16},{24,28},{28,24},{1,5},{5... | collective-permute-start | bytes 1572872 | tf_op jit(solution)/shard_map/ppermute | solution.py:1203
  (27 other events, 57.7 us)
